TPU v7x, 32 devices: a whole 2x2x4 slice. The times are simulated.
32 devices in a mesh: side: 4 (over z), rep: 8 (over y, x, core).
Axes of the slice: x: 2, y: 2, z: 4, core: 2. Of those that a mesh axis runs over, the one named last changes fastest.
Arguments:
- w_up: float32 [4, 1, 2048, 2816], P('side', None, 'rep')
- w_down: float32 [4, 1, 2816, 2048], P('side', None, None, 'rep')
- g_up: float32 [4, 1, 2048, 2816], P('side', None, 'rep')
- g_down: float32 [4, 1, 2816, 2048], P('side', None, None, 'rep')
- learn_rate: float32 [1], replicated
- old_up: bfloat16 [4, 8, 1, 2048, 2816], P('side', 'rep')
- old_down: bfloat16 [4, 8, 1, 2816, 2048], P('side', 'rep')
- prompts: bfloat16 [4, 8, 1024, 2048], P('side', 'rep')
Outputs:
- output 1: float32 [4, 1, 2048, 2816], P('side', None, 'rep')
- output 2: float32 [4, 1, 2816, 2048], P('side', None, None, 'rep')
- output 3: bfloat16 [4, 8, 1024, 2048], P('side', 'rep')
All inputs are finite; a program needn't handle non-finite values.
Results may differ from a plain program's by a relative error of at most 0.00721101.
Values are sent between devices in bfloat16 or wider.
A program may use at most 1 GiB of HBM per device.

v0:
```python
import jax
import jax.numpy as jnp
from jax import lax
from jax.sharding import PartitionSpec as P


def solution(mesh):
    tp_width = mesh.shape["side"] // 2
    send_pairs = [(slot_pos, slot_pos + tp_width) for slot_pos in range(tp_width)]
    up_spec = P("side", None, "rep", None)
    down_spec = P("side", None, None, "rep")
    copy_spec = P("side", "rep", None, None, None)
    token_spec = P("side", "rep", None, None)

    def local_step(w_up, w_down, g_up, g_down, learn_rate, old_up, old_down, prompts):
        step_rate = learn_rate[0]
        new_up = w_up - step_rate * g_up
        new_down = w_down - step_rate * g_down
        delta_up = (new_up - w_up)[0].astype(jnp.bfloat16)
        delta_down = (new_down - w_down)[0].astype(jnp.bfloat16)
        recv_up = lax.ppermute(delta_up, "side", send_pairs)
        recv_down = lax.ppermute(delta_down, "side", send_pairs)
        full_up = lax.all_gather(recv_up, "rep", axis=1, tiled=True)
        full_down = lax.all_gather(recv_down, "rep", axis=2, tiled=True)
        gen_up = (old_up[0, 0].astype(jnp.float32) + full_up.astype(jnp.float32)).astype(jnp.bfloat16)
        gen_down = (old_down[0, 0].astype(jnp.float32) + full_down.astype(jnp.float32)).astype(jnp.bfloat16)
        is_gen = lax.axis_index("side") >= tp_width
        gen_mask = is_gen.astype(jnp.float32)
        hidden = prompts[0, 0]
        for layer_idx in range(w_up.shape[1]):
            pre_act = jnp.dot(hidden, gen_up[layer_idx], preferred_element_type=jnp.float32)
            act_val = jax.nn.gelu(pre_act, approximate=False).astype(jnp.bfloat16)
            part_sum = jnp.dot(act_val, gen_down[layer_idx], preferred_element_type=jnp.float32)
            tp_total = lax.psum(part_sum * gen_mask, "side")
            hidden = (hidden.astype(jnp.float32) + tp_total).astype(jnp.bfloat16)
        y_local = jnp.where(is_gen, hidden, jnp.zeros_like(hidden))
        return new_up, new_down, y_local[None, None]

    return jax.shard_map(
        local_step,
        mesh=mesh,
        in_specs=(up_spec, down_spec, up_spec, down_spec, P(None), copy_spec, copy_spec, token_spec),
        out_specs=(up_spec, down_spec, token_spec),
        check_vma=False,
    )
```

profile of v0, /device:TPU:24, one launch (start us, length us, event | category | flops | bytes accessed | tf_op | source)
XLA Modules:
  0.0 573.4 jit_solution(391396328181216792)
XLA Ops:
  7.2 0.0 copy-start
  7.2 0.0 all-gather.3.cloned.1.call-start
  8.0 4.7 fusion.72
  12.7 1.3 collective-permute-start
  14.0 96.1 %collective-permute-done = bf16[1,256,2816]{2,1,0:T(8,128)(2,1)} collective-permute-done((bf16[1,256,2816]{2,1,0:T(8,128)(2,1)S(1)}, bf16[1,256,2816]{2,1,0:T(8,128)(2,1)}, u32[]{:S(2)}, u32[]{:S(2)}) %collective-permute-start) | collective-permute-done | bytes 1441824 | tf_op jit(solution)/shard_map/ppermute | solution.py:21
  110.1 0.0 all-gather.3.cloned.1.call-update
  110.2 0.0 all-gather.5.cloned.1.call-start
  110.2 0.0 copy-done
  110.2 3.9 fusion.73
  114.2 1.3 collective-permute-start.1
  115.5 35.2 %collective-permute-done.1 = bf16[1,2816,256]{2,1,0:T(8,128)(2,1)S(1)} collective-permute-done((bf16[1,2816,256]{2,1,0:T(8,128)(2,1)S(1)}, bf16[1,2816,256]{2,1,0:T(8,128)(2,1)S(1)}, u32[]{:S(2)}, u32[]{:S(2)}) %collective-permute-start.1) | collective-permute-done | bytes 1441824 | tf_op jit(solution)/shard_map/ppermute | solution.py:22
  150.6 0.0 copy-start.1
  150.6 1.1 copy-done.1
  151.7 0.0 all-gather.5.cloned.1.call-update
  151.7 0.0 all-reduce.2.cloned.1.call-start
  151.8 26.9 %all-gather.3.cloned.1.call-done = bf16[1,2048,2816]{2,1,0:T(8,128)(2,1)} async-done(((bf16[1,256,2816]{2,1,0:T(8,128)(2,1)}), bf16[1,2048,2816]{2,1,0:T(8,128)(2,1)}) %all-gather.3.cloned.1.call-update) | async-done | bytes 11534352 | tf_op jit(solution)/shard_map/all_gather | solution.py:23
  178.7 43.9 %fusion.4.clone.7 = bf16[1024,2816]{0,1:T(8,128)(2,1)} fusion(bf16[1,2048,2816]{2,1,0:T(8,128)(2,1)} %all-gather.3.cloned.1.call-done, bf16[1,1,1,2048,2816]{4,3,2,1,0:T(8,128)(2,1)} %param.13, bf16[1,1,1024,2048]{3,2,1,0:T(8,128)(2,1)} %param.15), kind=kOutput, calls=%fused_computation.7.clone.clone.clone.clone.clone.2 | convolution fusion | flops 12021661696 | bytes 33030144 | tf_op jit(solution)/shard_map/dot_general | solution.py:31
  222.6 28.2 %all-gather.5.cloned.1.call-done = bf16[1,2816,2048]{2,1,0:T(8,128)(2,1)} async-done(((bf16[1,2816,256]{2,1,0:T(8,128)(2,1)}), bf16[1,2816,2048]{2,1,0:T(8,128)(2,1)}) %all-gather.5.cloned.1.call-update) | async-done | bytes 11534352 | tf_op jit(solution)/shard_map/all_gather | solution.py:24
  250.8 20.5 %broadcast_multiply_fusion = f32[1024,2048]{1,0:T(8,128)} fusion(f32[]{:T(128)S(6)} %convert_element_type.94, bf16[1,2816,2048]{2,1,0:T(8,128)(2,1)} %all-gather.5.cloned.1.call-done, bf16[1,1,1,2816,2048]{4,3,2,1,0:T(8,128)(2,1)} %param.14, bf16[1024,2816]{0,1:T(8,128)(2,1)} %fusion.4.clone.7), kind=kOutput, calls=%fused_computation.68 | convolution fusion | flops 11836325888 | bytes 37224452 | tf_op jit(solution)/shard_map/dot_general | solution.py:33
  271.3 0.0 all-reduce.2.cloned.1.call-update
  271.3 287.2 %all-reduce.2.cloned.1.call-done = f32[1024,2048]{1,0:T(8,128)} async-done(((f32[1024,2048]{1,0:T(8,128)}), f32[1024,2048]{1,0:T(8,128)}) %all-reduce.2.cloned.1.call-update) | async-done | bytes 8388624 | tf_op jit(solution)/shard_map/psum | solution.py:34
  558.5 8.3 %fusion.63 = bf16[1,1,1024,2048]{3,2,1,0:T(8,128)(2,1)} fusion(f32[1024,2048]{1,0:T(8,128)} %all-reduce.2.cloned.1.call-done, bf16[1,1,1024,2048]{3,2,1,0:T(8,128)(2,1)} %param.15, pred[]{:T(512)S(6)} %ge.3), kind=kLoop, calls=%fused_computation.66 | loop fusion | flops 8388608 | bytes 16777216 | tf_op jit(solution)/shard_map/broadcast_in_dim | solution.py:37
Async XLA Ops:
  7.2 103.0 %copy-start = (f32[1,1,2816,256]{3,2,1,0:T(8,128)S(1)}, f32[1,1,2816,256]{3,2,1,0:T(8,128)}, u32[]{:S(2)}) copy-start(f32[1,1,2816,256]{3,2,1,0:T(8,128)} %param.9) | copy-start | bytes 8650756
  7.2 171.5 %all-gather.3.cloned.1.call-start = ((), (), s32[]{:S(2)}) async-start(), calls=%async_computation | async-start | bytes 12976128 | tf_op jit(solution)/shard_map/all_gather | solution.py:23
  12.7 97.4 %collective-permute-start = (bf16[1,256,2816]{2,1,0:T(8,128)(2,1)S(1)}, bf16[1,256,2816]{2,1,0:T(8,128)(2,1)}, u32[]{:S(2)}, u32[]{:S(2)}) collective-permute-start(bf16[1,256,2816]{2,1,0:T(8,128)(2,1)S(1)} %get-tuple-element.3), channel_id=1, source_target_pairs={{0,16},{8,24},{1,17},{9,25},{2,18},{10,26},{3,19},{11,27},{4,20},{... | collective-permute-start | bytes 4325384 | tf_op jit(solution)/shard_map/ppermute | solution.py:21
  110.2 140.7 %all-gather.5.cloned.1.call-start = ((), (), s32[]{:S(2)}) async-start(), calls=%async_computation.1 | async-start | bytes 12976128 | tf_op jit(solution)/shard_map/all_gather | solution.py:24
  114.2 36.5 %collective-permute-start.1 = (bf16[1,2816,256]{2,1,0:T(8,128)(2,1)S(1)}, bf16[1,2816,256]{2,1,0:T(8,128)(2,1)S(1)}, u32[]{:S(2)}, u32[]{:S(2)}) collective-permute-start(bf16[1,2816,256]{2,1,0:T(8,128)(2,1)S(1)} %get-tuple-element.5), channel_id=1, source_target_pairs={{0,16},{8,24},{1,17},{9,25},{2,18},{10,26},{3,19},{11,27},{4,20},{... | collective-permute-start | bytes 4325384 | tf_op jit(solution)/shard_map/ppermute | solution.py:22
  150.6 1.1 copy-start.1
  151.7 406.8 %all-reduce.2.cloned.1.call-start = ((), (), s32[]{:S(2)}) async-start(), calls=%async_computation.2 | async-start | bytes 16777216 | tf_op jit(solution)/shard_map/psum | solution.py:34
Sparse Core Ops, SparseCore 0:
  110.3 68.3 all-gather.2
  181.1 69.6 all-gather.4
  271.5 287.0 all-reduce.1
where the time goes:
time: 577 us; the launch traced here: 573 us
  waiting for transfers between devices  474 us (82%)
  matrix products  64.4 us (11%)
  other arithmetic  17 us (3%)
  between operations  14.6 us (3%)
    psum x1, waiting for transfers between devices, local_step(): tp_total = lax.psum(part_sum * gen_mask, 'side')  287 us
    ppermute x1, waiting for transfers between devices, local_step(): recv_up = lax.ppermute(delta_up, 'side', send_pairs)  96.1 us
    dot_general x1, matrix products, local_step(): jnp.dot(hidden, gen_up[layer_idx], preferred_element_type=jnp.float32)  43.9 us
    ppermute x1, waiting for transfers between devices, local_step(): recv_down = lax.ppermute(delta_down, 'side', send_pairs)  35.2 us
    all_gather x1, waiting for transfers between devices, local_step(): full_down = lax.all_gather(recv_down, 'rep', axis=2, tiled=True)  28.2 us
    all_gather x1, waiting for transfers between devices, local_step(): full_up = lax.all_gather(recv_up, 'rep', axis=1, tiled=True)  26.9 us
    dot_general x1, matrix products, local_step(): jnp.dot(act_val, gen_down[layer_idx], preferred_element_type=jnp.float32)  20.5 us
  transfers between devices with their start and end apart: 5, of which 5 were waited for; matrix products, arithmetic and copies ran while one was open for 8% of the time, Pallas kernels for 0%

commit v1 on v0

v1 whole, which is shorter than its diff:
```python
import functools

import jax
import jax.numpy as jnp
from jax import lax
from jax.experimental import pallas as pl
from jax.experimental.pallas import tpu as pltpu
from jax.sharding import PartitionSpec as P

MESH = pl.DeviceIdType.MESH
F32 = jnp.float32
BF16 = jnp.bfloat16
DX, DY, DZ = 1, 2, 4
STAGES = 4


def exact_gelu(v):
    return (0.5 * v) * (1.0 + lax.erf(v * (0.5**0.5)))


def sync_kernel(
    n_chunks, width, rows, up_delta, down_delta, old_up, old_down, prompts, y_ref,
    weights, acc, hidden, stale,
    up_recv, down_recv, send_sem, recv_sem, pair_recv, stale_sem, io_sem, pace_sem,
):
    side = lax.axis_index("side")
    rep = lax.axis_index("rep")
    core = rep % 2
    xpos = (rep // 2) % 2
    ypos = rep // 4
    is_gen = side >= 2
    rank = side % 2
    tokens = hidden.shape[0]

    barrier = pltpu.get_barrier_semaphore()

    def ping(sem, to_side, to_rep):
        pl.semaphore_signal(sem, inc=1, device_id=(to_side, to_rep), device_id_type=MESH)

    x_rep = rep + 2 * (1 - 2 * xpos)
    y_rep = rep + 4 * (1 - 2 * ypos)
    pair_rep = rep + (1 - 2 * core)
    z_side = 5 - side

    def columns(c):
        return pl.ds(pl.multiple_of(c * width, width), width)

    mine = pl.ds(pl.multiple_of(rep * rows, rows), rows)

    def delta_copies(c, to_side):
        slot = weights.at[c, rank, rep // 2, core]
        up = pltpu.make_async_remote_copy(
            src_ref=up_delta.at[:, columns(c)], dst_ref=slot.at[0], send_sem=send_sem.at[c, 0],
            recv_sem=up_recv.at[c], device_id=(to_side, rep), device_id_type=MESH,
        )
        down = pltpu.make_async_remote_copy(
            src_ref=down_delta.at[columns(c), :], dst_ref=slot.at[1], send_sem=send_sem.at[c, 1],
            recv_sem=down_recv.at[c], device_id=(to_side, rep), device_id_type=MESH,
        )
        return up, down

    def prompts_in():
        return pltpu.make_async_copy(prompts.at[0, 0], hidden, io_sem.at[0])

    def result_out():
        return pltpu.make_async_copy(hidden, y_ref.at[0, 0], io_sem.at[1])

    @pl.when(side < 2)
    def _():
        prompts_in().start()
        ping(barrier, side + 2, rep)
        ping(barrier, 1 - side, rep)
        pl.semaphore_wait(barrier, 2)

        def send(c, carry):
            @pl.when((side == 0) & (c >= 1))
            def _():
                pl.semaphore_wait(pace_sem, 1)

            for copy in delta_copies(c, side + 2):
                copy.start()

            @pl.when((side == 1) & (c >= 1))
            def _():
                for copy in delta_copies(c - 1, side + 2):
                    copy.wait_send()
                ping(pace_sem, 0, rep)

            return carry

        lax.fori_loop(0, n_chunks, send, 0)

        @pl.when(side == 1)
        def _():
            for copy in delta_copies(n_chunks - 1, side + 2):
                copy.wait_send()

        @pl.when(side == 0)
        def _():
            def drain(c, carry):
                for copy in delta_copies(c, side + 2):
                    copy.wait_send()
                return carry

            lax.fori_loop(0, n_chunks, drain, 0)

        prompts_in().wait()
        result_out().start()
        result_out().wait()

    @pl.when(is_gen)
    def _():
        prompts_in().start()

        def slot_at(d):
            t = 1 - rank if d & DZ else rank
            yy = 1 - ypos if d & DY else ypos
            xx = 1 - xpos if d & DX else xpos
            return t, yy * 2 + xx

        def stale_copies(c):
            up = pltpu.make_async_copy(
                old_up.at[0, 0, 0, mine, columns(c)], stale.at[c % 2, 0], stale_sem.at[c % 2, 0]
            )
            down = pltpu.make_async_copy(
                old_down.at[0, 0, 0, columns(c), mine], stale.at[c % 2, 1], stale_sem.at[c % 2, 1]
            )
            return up, down

        def message(c, d, axis, send_slot):
            t, yx = slot_at(d)
            ref = weights.at[c, t, yx, core]
            if axis == DX:
                to = (side, x_rep)
            elif axis == DY:
                to = (side, y_rep)
            else:
                to = (z_side, rep)
            return pltpu.make_async_remote_copy(
                src_ref=ref, dst_ref=ref, send_sem=send_sem.at[c, send_slot], recv_sem=recv_sem.at[c, d | axis],
                device_id=to, device_id_type=MESH,
            )

        def arrival(c, d):
            t, yx = slot_at(d)
            ref = weights.at[c, t, yx, core]
            return pltpu.make_async_remote_copy(
                src_ref=ref, dst_ref=ref, send_sem=send_sem.at[c, 0], recv_sem=recv_sem.at[c, d],
                device_id=(side, rep), device_id_type=MESH,
            )

        def pair_message(c, dz):
            t = 1 - rank if dz else rank
            ref = weights.at[c, t, :, core]
            return pltpu.make_async_remote_copy(
                src_ref=ref, dst_ref=ref, send_sem=send_sem.at[c, 7 + dz], recv_sem=pair_recv.at[c, dz],
                device_id=(side, pair_rep), device_id_type=MESH,
            )

        def pair_arrival(c, dz):
            t = 1 - rank if dz else rank
            ref = weights.at[c, t, :, 1 - core]
            return pltpu.make_async_remote_copy(
                src_ref=ref, dst_ref=ref, send_sem=send_sem.at[c, 0], recv_sem=pair_recv.at[c, dz],
                device_id=(side, pair_rep), device_id_type=MESH,
            )

        for c in (0, 1):
            for copy in stale_copies(c):
                copy.start()
        ping(barrier, side, x_rep)
        ping(barrier, side, y_rep)
        ping(barrier, side, pair_rep)
        ping(barrier, z_side, rep)
        ping(barrier, side - 2, rep)

        def clear(i, carry):
            acc[pl.ds(pl.multiple_of(i * 64, 64), 64), :] = jnp.zeros((64, acc.shape[1]), F32)
            return carry

        lax.fori_loop(0, tokens // 64, clear, 0)
        pl.semaphore_wait(barrier, 5)
        prompts_in().wait()

        def odd(c):
            return c % 2 == 1

        def via_x(c):
            return c % 5 == 1

        def via_y(c):
            return c % 5 == 4

        def via_z(c):
            return (c % 5 != 1) & (c % 5 != 4)

        hop1 = ((0, DX, 0, None), (0, DY, 1, None), (0, DZ, 2, None))
        hop2 = (
            (DZ, DX, 3, None),
            (DZ, DY, 4, None),
            (DY, DX, 5, lambda c: c % 2 == 0),
            (DX, DY, 5, odd),
        )
        hop3 = ((DY | DZ, DX, 6, via_x), (DX | DZ, DY, 6, via_y), (DX | DY, DZ, 6, via_z))

        def send_all(c, routes):
            for d, axis, send_slot, which in routes:
                if which is None:
                    message(c, d, axis, send_slot).start()
                else:

                    @pl.when(which(c))
                    def _(d=d, axis=axis, send_slot=send_slot):
                        message(c, d, axis, send_slot).start()

        def own_chunk(c):
            slot = weights.at[c, rank, rep // 2, core]
            for half, sem in ((0, up_recv), (1, down_recv)):
                pltpu.make_async_remote_copy(
                    src_ref=slot.at[half], dst_ref=slot.at[half], send_sem=send_sem.at[c, 0], recv_sem=sem.at[c],
                    device_id=(side - 2, rep), device_id_type=MESH,
                ).wait_recv()
            for copy in stale_copies(c):
                copy.wait()
            for half in (0, 1):
                slot[half] = (stale[c % 2, half].astype(F32) + slot[half].astype(F32)).astype(BF16)

            @pl.when(c + 2 < n_chunks)
            def _():
                for copy in stale_copies(c + 2):
                    copy.start()

        block = min(512, tokens)

        def multiply(c, t):
            def body(m, carry):
                here = pl.ds(pl.multiple_of(m * block, block), block)
                up_mat = weights[c, t, :, :, 0].reshape(8 * rows, width)
                pre_act = jnp.dot(hidden[here, :], up_mat, preferred_element_type=F32)
                act = exact_gelu(pre_act).astype(BF16)
                for piece in range(8):
                    cols = slice(piece * rows, (piece + 1) * rows)
                    acc[here, cols] += jnp.dot(
                        act, weights[c, t, piece // 2, piece % 2, 1], preferred_element_type=F32
                    )
                return carry

            lax.fori_loop(0, tokens // block, body, 0)

        def step(i, carry):
            @pl.when(i < n_chunks)
            def _():
                own_chunk(i)

            @pl.when((i >= 1) & (i < n_chunks + 1))
            def _():
                for d in (DX, DY, DZ):
                    arrival(i - 1, d).wait_recv()
                send_all(i - 1, hop2)

            @pl.when(i < n_chunks)
            def _():
                send_all(i, hop1)

            @pl.when((i >= 2) & (i < n_chunks + 2))
            def _():
                for d in (DX | DY, DX | DZ, DY | DZ):
                    arrival(i - 2, d).wait_recv()
                send_all(i - 2, hop3)
                pair_message(i - 2, 0).start()

            @pl.when((i >= 3) & (i < n_chunks + 3))
            def _():
                arrival(i - 3, DX | DY | DZ).wait_recv()
                pair_message(i - 3, 1).start()

            @pl.when(i >= STAGES)
            def _():
                c = i - STAGES
                for dz in (0, 1):
                    pair_arrival(c, dz).wait_recv()

                def ranks(t, carry):
                    multiply(c, t)
                    return carry

                lax.fori_loop(0, 2, ranks, 0)

            return carry

        lax.fori_loop(0, n_chunks + STAGES, step, 0)

        def finish(m, carry):
            here = pl.ds(pl.multiple_of(m * 64, 64), 64)
            hidden[here, :] = (hidden[here, :].astype(F32) + acc[here, :]).astype(BF16)
            return carry

        lax.fori_loop(0, tokens // 64, finish, 0)
        result_out().start()

        def drain(c, carry):
            for d, axis, send_slot, _ in hop1 + hop2[:3] + hop3[:1]:
                message(c, d, axis, send_slot).wait_send()
            for dz in (0, 1):
                pair_message(c, dz).wait_send()
            return carry

        lax.fori_loop(0, n_chunks, drain, 0)
        result_out().wait()


def solution(mesh):
    up_spec = P("side", None, "rep", None)
    down_spec = P("side", None, None, "rep")
    copy_spec = P("side", "rep", None, None, None)
    token_spec = P("side", "rep", None, None)

    def local_step(w_up, w_down, g_up, g_down, learn_rate, old_up, old_down, prompts):
        step_rate = learn_rate[0]
        new_up = w_up - step_rate * g_up
        new_down = w_down - step_rate * g_down
        delta_up = (new_up - w_up)[0, 0].astype(BF16)
        delta_down = (new_down - w_down)[0, 0].astype(BF16)
        rows, shard = delta_up.shape
        width = 256 if shard % 256 == 0 else 128
        n_chunks = shard // width
        tokens, model = prompts.shape[2:]
        y = pl.pallas_call(
            functools.partial(sync_kernel, n_chunks, width, rows),
            out_shape=jax.ShapeDtypeStruct(prompts.shape, BF16),
            in_specs=[pl.BlockSpec(memory_space=pl.ANY)] * 5,
            out_specs=pl.BlockSpec(memory_space=pl.ANY),
            scratch_shapes=[
                pltpu.VMEM((n_chunks, 2, 4, 2, 2, rows, width), BF16),
                pltpu.VMEM((tokens, model), F32),
                pltpu.VMEM((tokens, model), BF16),
                pltpu.VMEM((2, 2, rows, width), BF16),
                pltpu.SemaphoreType.DMA((n_chunks,)),
                pltpu.SemaphoreType.DMA((n_chunks,)),
                pltpu.SemaphoreType.DMA((n_chunks, 9)),
                pltpu.SemaphoreType.DMA((n_chunks, 8)),
                pltpu.SemaphoreType.DMA((n_chunks, 2)),
                pltpu.SemaphoreType.DMA((2, 2)),
                pltpu.SemaphoreType.DMA((2,)),
                pltpu.SemaphoreType.REGULAR,
            ],
            compiler_params=pltpu.CompilerParams(
                collective_id=0, has_side_effects=True, vmem_limit_bytes=67043328
            ),
        )(delta_up, delta_down, old_up, old_down, prompts)
        return new_up, new_down, y

    return jax.shard_map(
        local_step,
        mesh=mesh,
        in_specs=(up_spec, down_spec, up_spec, down_spec, P(None), copy_spec, copy_spec, token_spec),
        out_specs=(up_spec, down_spec, token_spec),
        check_vma=False,
    )
```

time: 577 us -> 260 us (0.45)
  waiting for transfers between devices: 474 us -> 0 us
  Pallas kernels: 0 us -> 245 us
  matrix products: 64.4 us -> 0 us
  between operations: 14.6 us -> 1.3 us
  other arithmetic: 17 us -> 8 us
    psum x1 -> x0, waiting for transfers between devices: 287 us -> none  [local_step(): tp_total = lax.psum(part_sum * gen_mask, 'side')]
    pallas_call x0 -> x1, Pallas kernels: none -> 245 us  [local_step(): pl.pallas_call(functools.partial(sync_kernel, n_chunks, width, rows), out...]
    ppermute x2 -> x0, waiting for transfers between devices: 131 us -> none  [the longest x1 96.1 us: local_step(): recv_up = lax.ppermute(delta_up, 'side', send_pairs)]
    dot_general x2 -> x0, matrix products: 64.4 us -> none  [the longest x1 43.9 us: local_step(): jnp.dot(hidden, gen_up[layer_idx], preferred_element_type=jnp.float32)]
    all_gather x2 -> x0, waiting for transfers between devices: 55.1 us -> none  [the longest x1 28.2 us: local_step(): full_down = lax.all_gather(recv_down, 'rep', axis=2, tiled=True)]
    broadcast_in_dim x1 -> x0, other arithmetic: 8.32 us -> none  [local_step(): return (new_up, new_down, y_local[None, None])]
  transfers between devices with their start and end apart: 5 -> 0, of which waited for: 5 -> 0; matrix products, arithmetic and copies ran while one was open for 8% -> 0% of each run, Pallas kernels for 0% -> 0%
where the time goes in v1:
time: 260 us
  Pallas kernels  245 us (94%)
  other arithmetic  8 us (3%)
  local copies, waits for them, and re-layouts  4.8 us (2%)
    pallas_call x1, Pallas kernels, local_step(): pl.pallas_call(functools.partial(sync_kernel, n_chunks, width, rows), out...  245 us
    convert_element_type x1, other arithmetic, local_step(): delta_up = (new_up - w_up)[0, 0].astype(BF16)  5.28 us

profile of v1, /device:TPU:24, one launch (start us, length us, event | category | flops | bytes accessed | tf_op | source)
XLA Modules:
  0.0 259.5 jit_solution(9506546931823905080)
XLA Ops:
  1.3 0.0 copy-start
  1.3 0.0 copy-start.1
  1.3 5.3 %fusion = (bf16[256,2816]{1,0:T(8,128)(2,1)}, f32[1,1,256,2816]{3,2,1,0:T(8,128)}) fusion(f32[1,1,256,2816]{3,2,1,0:T(8,128)} %param.8, f32[1,1,256,2816]{3,2,1,0:T(8,128)} %param.10, f32[]{:T(128)} %bitcast.5), kind=kLoop, calls=%fused_computation.4 | loop fusion | flops 2883584 | bytes 10092548 | tf_op jit(solution)/shard_map/convert_element_type | solution.py:322
  6.6 0.0 copy-done
  6.6 0.0 copy-done.1
  6.6 2.7 %fusion.1 = (bf16[2816,256]{1,0:T(8,128)(2,1)}, f32[1,1,2816,256]{3,2,1,0:T(8,128)}) fusion(f32[1,1,2816,256]{3,2,1,0:T(8,128)S(1)} %copy-done, f32[1,1,2816,256]{3,2,1,0:T(8,128)S(1)} %copy-done.1, f32[]{:T(128)} %bitcast.6), kind=kLoop, calls=%fused_computation.5 | loop fusion | flops 2883584 | bytes 10092548 | tf_op jit(solution)/shard_map/convert_element_type | solution.py:323
  9.3 245.4 %shard_map.103 = bf16[1,1,1024,2048]{3,2,1,0:T(8,128)(2,1)} custom-call(bf16[256,2816]{1,0:T(8,128)(2,1)} %get-tuple-element.5.up_delta, bf16[2816,256]{1,0:T(8,128)(2,1)} %get-tuple-element.3.down_delta, bf16[1,1,1,2048,2816]{4,3,2,1,0:T(8,128)(2,1)} %old_up.1, bf16[1,1,1,2816,2048]{4,3,2,1,0:T(8,128)(2,1)} %old_down.1, bf16[1,1,1024,2048]{3,2,1,0:T(8,128)(2,1)} %prompts.1), custom_call_target="tpu_custom_call" | custom-call | tf_op jit(solution)/shard_map/pallas_call | solution.py:328
  254.7 4.8 %copy.13 = bf16[1,1,1024,2048]{3,2,1,0:T(8,128)(2,1)} copy(bf16[1,1,1024,2048]{3,2,1,0:T(8,128)(2,1)} %shard_map.103) | data formatting | bytes 8388608
Async XLA Ops:
  1.3 5.3 %copy-start = (f32[1,1,2816,256]{3,2,1,0:T(8,128)S(1)}, f32[1,1,2816,256]{3,2,1,0:T(8,128)}, u32[]{:S(2)}) copy-start(f32[1,1,2816,256]{3,2,1,0:T(8,128)} %param.9) | copy-start | bytes 8650756
  1.3 5.3 %copy-start.1 = (f32[1,1,2816,256]{3,2,1,0:T(8,128)S(1)}, f32[1,1,2816,256]{3,2,1,0:T(8,128)}, u32[]{:S(2)}) copy-start(f32[1,1,2816,256]{3,2,1,0:T(8,128)} %param.11) | copy-start | bytes 8650756

commit v2 on v0

v2 whole, which is shorter than its diff:
```python
import functools

import jax
import jax.numpy as jnp
from jax import lax
from jax.experimental import pallas as pl
from jax.experimental.pallas import tpu as pltpu
from jax.sharding import PartitionSpec as P

MESH = pl.DeviceIdType.MESH
F32 = jnp.float32
BF16 = jnp.bfloat16
LANES = 128
DX, DY, DZ = 1, 2, 4
WHOLE, UPPER, LOWER = (0, 4), (0, 2), (2, 4)
ARRIVALS = {
    (DX, WHOLE): 0, (DY, WHOLE): 1, (DZ, WHOLE): 2, (DX | DZ, WHOLE): 3, (DY | DZ, WHOLE): 4,
    (DX | DY, UPPER): 5, (DX | DY, LOWER): 6, (DX | DY | DZ, WHOLE): 7,
}
HOP1 = ((0, DZ, WHOLE), (0, DX, WHOLE), (0, DY, WHOLE))
HOP2 = ((DZ, DX, WHOLE), (DZ, DY, WHOLE), (DY, DX, UPPER), (DX, DY, LOWER))
HOP3 = ((DX | DY, DZ, WHOLE),)
SENDS = HOP1 + HOP2 + HOP3
N_SEMS = len(SENDS) + 2
WINDOW = 6
PACE = 2
LAST = 4


def exact_gelu(v):
    return (0.5 * v) * (1.0 + lax.erf(v * (0.5**0.5)))


def sync_kernel(
    n_chunks, up_delta, down_delta, old_up, old_down, prompts, y_ref,
    weights, acc, hidden, stale,
    own_recv, send_sem, recv_sem, pair_recv, stale_sem, io_sem, pace_sem, credit_sem,
):
    side = lax.axis_index("side")
    rep = lax.axis_index("rep")
    core = rep % 2
    xpos = (rep // 2) % 2
    ypos = rep // 4
    rank = side % 2
    tokens = hidden.shape[0]
    rows = 2 * LANES

    barrier = pltpu.get_barrier_semaphore()

    def ping(sem, to_side, to_rep):
        pl.semaphore_signal(sem, inc=1, device_id=(to_side, to_rep), device_id_type=MESH)

    x_rep = rep + 2 * (1 - 2 * xpos)
    y_rep = rep + 4 * (1 - 2 * ypos)
    pair_rep = rep + (1 - 2 * core)
    z_side = 5 - side

    def columns(c):
        return pl.ds(pl.multiple_of(c * LANES, LANES), LANES)

    def prompts_in():
        return pltpu.make_async_copy(prompts.at[0, 0], hidden, io_sem.at[0])

    @pl.when(side < 2)
    def _():
        def delta_copies(c):
            slot = weights.at[c, rank, rep // 2, core]

            def copy(src, dst, i):
                return pltpu.make_async_remote_copy(
                    src_ref=src, dst_ref=dst, send_sem=send_sem.at[c % WINDOW, i], recv_sem=own_recv.at[c, i],
                    device_id=(side + 2, rep), device_id_type=MESH,
                )

            return (
                [copy(up_delta.at[pl.ds(i * LANES, LANES), columns(c)], slot.at[i], i) for i in (0, 1)]
                + [copy(down_delta.at[columns(c), pl.ds(i * LANES, LANES)], slot.at[2 + i], 2 + i) for i in (0, 1)]
            )

        prompts_in().start()
        ping(barrier, side + 2, rep)
        ping(barrier, 1 - side, rep)
        pl.semaphore_wait(barrier, 2)

        def sent(c):
            for copy in delta_copies(c):
                copy.wait_send()

        def send(c, carry):
            @pl.when(c >= PACE)
            def _():
                pl.semaphore_wait(credit_sem, 1)

            @pl.when((side == 0) & (c >= 1))
            def _():
                pl.semaphore_wait(pace_sem, 1)

            for copy in delta_copies(c):
                copy.start()

            @pl.when(c >= 1)
            def _():
                sent(c - 1)

            @pl.when((side == 1) & (c >= 1))
            def _():
                ping(pace_sem, 0, rep)

            return carry

        lax.fori_loop(0, n_chunks, send, 0)
        sent(n_chunks - 1)
        prompts_in().wait()
        out = pltpu.make_async_copy(hidden, y_ref.at[0, 0], io_sem.at[1])
        out.start()
        out.wait()

    @pl.when(side >= 2)
    def _():
        prompts_in().start()

        def place(d):
            t = 1 - rank if d & DZ else rank
            yy = 1 - ypos if d & DY else ypos
            xx = 1 - xpos if d & DX else xpos
            return t, yy * 2 + xx

        def stale_copies(c):
            slot = stale.at[c % 2]
            first = pl.multiple_of(rep * rows, rows)

            def part(i):
                return pl.ds(first + i * LANES, LANES)

            return [
                pltpu.make_async_copy(old_up.at[0, 0, 0, part(i), columns(c)], slot.at[i], stale_sem.at[c % 2, i])
                for i in (0, 1)
            ] + [
                pltpu.make_async_copy(
                    old_down.at[0, 0, 0, columns(c), part(i)], slot.at[2 + i], stale_sem.at[c % 2, 2 + i]
                )
                for i in (0, 1)
            ]

        def blocks_of(c, d, blocks):
            t, yx = place(d)
            return weights.at[c, t, yx, core, pl.ds(blocks[0], blocks[1] - blocks[0])]

        def message(c, i):
            d, axis, blocks = SENDS[i]
            ref = blocks_of(c, d, blocks)
            to = {DX: (side, x_rep), DY: (side, y_rep), DZ: (z_side, rep)}[axis]
            return pltpu.make_async_remote_copy(
                src_ref=ref, dst_ref=ref, send_sem=send_sem.at[c % WINDOW, i],
                recv_sem=recv_sem.at[c, ARRIVALS[d | axis, blocks]], device_id=to, device_id_type=MESH,
            )

        def arrived(c, d, blocks):
            ref = blocks_of(c, d, blocks)
            pltpu.make_async_remote_copy(
                src_ref=ref, dst_ref=ref, send_sem=send_sem.at[0, 0], recv_sem=recv_sem.at[c, ARRIVALS[d, blocks]],
                device_id=(side, rep), device_id_type=MESH,
            ).wait_recv()

        def pair_message(c, dz, of_core):
            t = 1 - rank if dz else rank
            ref = weights.at[c, t, :, of_core]
            return pltpu.make_async_remote_copy(
                src_ref=ref, dst_ref=ref, send_sem=send_sem.at[c % WINDOW, len(SENDS) + dz],
                recv_sem=pair_recv.at[c, dz], device_id=(side, pair_rep), device_id_type=MESH,
            )

        for c in (0, 1):
            for copy in stale_copies(c):
                copy.start()
        ping(barrier, side, x_rep)
        ping(barrier, side, y_rep)
        ping(barrier, side, pair_rep)
        ping(barrier, z_side, rep)
        ping(barrier, side - 2, rep)

        def clear(i, carry):
            acc[pl.ds(pl.multiple_of(i * 64, 64), 64), :] = jnp.zeros((64, acc.shape[1]), F32)
            return carry

        lax.fori_loop(0, tokens // 64, clear, 0)
        pl.semaphore_wait(barrier, 5)
        prompts_in().wait()

        def send_all(c, first, last):
            for i in range(first, last):
                message(c, i).start()

        def add_own(c):
            slot = weights.at[c, rank, rep // 2, core]
            for i in range(4):
                pltpu.make_async_remote_copy(
                    src_ref=slot.at[i], dst_ref=slot.at[i], send_sem=send_sem.at[0, 0], recv_sem=own_recv.at[c, i],
                    device_id=(side - 2, rep), device_id_type=MESH,
                ).wait_recv()
            for copy in stale_copies(c):
                copy.wait()
            for i in range(4):
                slot[i] = (stale[c % 2, i].astype(F32) + slot[i].astype(F32)).astype(BF16)

            @pl.when(c + PACE < n_chunks)
            def _():
                ping(credit_sem, side - 2, rep)

            @pl.when(c + 2 < n_chunks)
            def _():
                for copy in stale_copies(c + 2):
                    copy.start()

        half = tokens // 2

        def multiply(c, m):
            here = slice(m * half, (m + 1) * half)
            up_mat = jnp.concatenate(
                [weights[c, t, :, :, 0:2].reshape(acc.shape[1], LANES) for t in (0, 1)], axis=1
            )
            pre_act = jnp.dot(hidden[here, :], up_mat, preferred_element_type=F32)
            act = exact_gelu(pre_act).astype(BF16)
            for piece in range(8):
                down_mat = jnp.concatenate(
                    [
                        jnp.concatenate([weights[c, t, piece // 2, piece % 2, 2 + i] for i in (0, 1)], axis=1)
                        for t in (0, 1)
                    ],
                    axis=0,
                )
                acc[here, piece * rows : (piece + 1) * rows] += jnp.dot(act, down_mat, preferred_element_type=F32)

        def drain(c):
            for i in range(len(SENDS)):
                message(c, i).wait_send()
            for dz in (0, 1):
                pair_message(c, dz, core).wait_send()

        def step(i, carry):
            def during(lag, upto=None):
                if upto is None:
                    return pl.when((i >= lag) & (i < n_chunks + lag))
                return pl.when((i >= lag) & (i < upto + lag))

            @during(0)
            def _():
                add_own(i)
                send_all(i, 0, len(HOP1))

            @during(1)
            def _():
                arrived(i - 1, DZ, WHOLE)
                send_all(i - 1, 3, 5)
                arrived(i - 1, DX, WHOLE)
                arrived(i - 1, DY, WHOLE)
                send_all(i - 1, 5, 7)

            @during(LAST)
            def _():
                for dz in (0, 1):
                    pair_message(i - LAST, dz, 1 - core).wait_recv()
                multiply(i - LAST, 0)

            @during(2)
            def _():
                c = i - 2
                arrived(c, DX | DY, UPPER)
                arrived(c, DX | DY, LOWER)
                send_all(c, 7, len(SENDS))
                pair_message(c, 0, core).start()
                arrived(c, DX | DZ, WHOLE)
                arrived(c, DY | DZ, WHOLE)

            @during(3)
            def _():
                arrived(i - 3, DX | DY | DZ, WHOLE)
                pair_message(i - 3, 1, core).start()

            @during(LAST)
            def _():
                multiply(i - LAST, 1)

            @pl.when((i >= WINDOW - 1) & (i < n_chunks + WINDOW - 1))
            def _():
                drain(i - (WINDOW - 1))

            return carry

        lax.fori_loop(0, n_chunks + LAST, step, 0)
        for c in range(n_chunks + LAST - (WINDOW - 1), n_chunks):
            drain(c)

        finish_rows = tokens // 4

        def result_out(m):
            here = pl.ds(pl.multiple_of(m * finish_rows, finish_rows), finish_rows)
            return pltpu.make_async_copy(hidden.at[here, :], y_ref.at[0, 0, here, :], io_sem.at[m])

        def finish(m, carry):
            here = pl.ds(pl.multiple_of(m * finish_rows, finish_rows), finish_rows)
            hidden[here, :] = (hidden[here, :].astype(F32) + acc[here, :]).astype(BF16)
            result_out(m).start()
            return carry

        lax.fori_loop(0, 4, finish, 0)
        for m in range(4):
            result_out(m).wait()


def solution(mesh):
    up_spec = P("side", None, "rep", None)
    down_spec = P("side", None, None, "rep")
    copy_spec = P("side", "rep", None, None, None)
    token_spec = P("side", "rep", None, None)

    def local_step(w_up, w_down, g_up, g_down, learn_rate, old_up, old_down, prompts):
        step_rate = learn_rate[0]
        new_up = w_up - step_rate * g_up
        new_down = w_down - step_rate * g_down
        delta_up = (new_up - w_up)[0, 0].astype(BF16)
        delta_down = (new_down - w_down)[0, 0].astype(BF16)
        n_chunks = delta_up.shape[1] // LANES
        tokens, model = prompts.shape[2:]
        y = pl.pallas_call(
            functools.partial(sync_kernel, n_chunks),
            out_shape=jax.ShapeDtypeStruct(prompts.shape, BF16),
            in_specs=[pl.BlockSpec(memory_space=pl.ANY)] * 5,
            out_specs=pl.BlockSpec(memory_space=pl.ANY),
            scratch_shapes=[
                pltpu.VMEM((n_chunks, 2, 4, 2, 4, LANES, LANES), BF16),
                pltpu.VMEM((tokens, model), F32),
                pltpu.VMEM((tokens, model), BF16),
                pltpu.VMEM((2, 4, LANES, LANES), BF16),
                pltpu.SemaphoreType.DMA((n_chunks, 4)),
                pltpu.SemaphoreType.DMA((WINDOW, N_SEMS)),
                pltpu.SemaphoreType.DMA((n_chunks, len(ARRIVALS))),
                pltpu.SemaphoreType.DMA((n_chunks, 2)),
                pltpu.SemaphoreType.DMA((2, 4)),
                pltpu.SemaphoreType.DMA((4,)),
                pltpu.SemaphoreType.REGULAR,
                pltpu.SemaphoreType.REGULAR,
            ],
            compiler_params=pltpu.CompilerParams(
                collective_id=0, has_side_effects=True, vmem_limit_bytes=67043328
            ),
        )(delta_up, delta_down, old_up, old_down, prompts)
        return new_up, new_down, y

    return jax.shard_map(
        local_step,
        mesh=mesh,
        in_specs=(up_spec, down_spec, up_spec, down_spec, P(None), copy_spec, copy_spec, token_spec),
        out_specs=(up_spec, down_spec, token_spec),
        check_vma=False,
    )
```

time: 577 us -> 223 us (0.39)
  waiting for transfers between devices: 474 us -> 0 us
  Pallas kernels: 0 us -> 208 us
  matrix products: 64.4 us -> 0 us
  between operations: 14.6 us -> 1.3 us
  other arithmetic: 17 us -> 8 us
    psum x1 -> x0, waiting for transfers between devices: 287 us -> none  [local_step(): tp_total = lax.psum(part_sum * gen_mask, 'side')]
    pallas_call x0 -> x1, Pallas kernels: none -> 208 us  [local_step(): pl.pallas_call(functools.partial(sync_kernel, n_chunks), out_shape=jax.Sh...]
    ppermute x2 -> x0, waiting for transfers between devices: 131 us -> none  [the longest x1 96.1 us: local_step(): recv_up = lax.ppermute(delta_up, 'side', send_pairs)]
    dot_general x2 -> x0, matrix products: 64.4 us -> none  [the longest x1 43.9 us: local_step(): jnp.dot(hidden, gen_up[layer_idx], preferred_element_type=jnp.float32)]
    all_gather x2 -> x0, waiting for transfers between devices: 55.1 us -> none  [the longest x1 28.2 us: local_step(): full_down = lax.all_gather(recv_down, 'rep', axis=2, tiled=True)]
    broadcast_in_dim x1 -> x0, other arithmetic: 8.32 us -> none  [local_step(): return (new_up, new_down, y_local[None, None])]
  transfers between devices with their start and end apart: 5 -> 0, of which waited for: 5 -> 0; matrix products, arithmetic and copies ran while one was open for 8% -> 0% of each run, Pallas kernels for 0% -> 0%
where the time goes in v2:
time: 223 us; the launch traced here: 222 us
  Pallas kernels  208 us (93%)
  other arithmetic  8 us (4%)
  local copies, waits for them, and re-layouts  4.8 us (2%)
    pallas_call x1, Pallas kernels, local_step(): pl.pallas_call(functools.partial(sync_kernel, n_chunks), out_shape=jax.Sh...  208 us
    convert_element_type x1, other arithmetic, local_step(): delta_up = (new_up - w_up)[0, 0].astype(BF16)  5.28 us
    unnamed x5, local copies, waits for them, and re-layouts  4.8 us

profile of v2, /device:TPU:24, one launch (start us, length us, event | category | flops | bytes accessed | tf_op | source)
XLA Modules:
  0.0 221.7 jit_solution(3222506089577755250)
XLA Ops:
  1.3 0.0 copy-start
  1.3 0.0 copy-start.1
  1.3 5.3 %fusion = (bf16[256,2816]{1,0:T(8,128)(2,1)}, f32[1,1,256,2816]{3,2,1,0:T(8,128)}) fusion(f32[1,1,256,2816]{3,2,1,0:T(8,128)} %param.8, f32[1,1,256,2816]{3,2,1,0:T(8,128)} %param.10, f32[]{:T(128)} %bitcast.5), kind=kLoop, calls=%fused_computation.4 | loop fusion | flops 2883584 | bytes 10092548 | tf_op jit(solution)/shard_map/convert_element_type | solution.py:321
  6.6 0.0 copy-done
  6.6 0.0 copy-done.1
  6.6 2.7 %fusion.1 = (bf16[2816,256]{1,0:T(8,128)(2,1)}, f32[1,1,2816,256]{3,2,1,0:T(8,128)}) fusion(f32[1,1,2816,256]{3,2,1,0:T(8,128)S(1)} %copy-done, f32[1,1,2816,256]{3,2,1,0:T(8,128)S(1)} %copy-done.1, f32[]{:T(128)} %bitcast.6), kind=kLoop, calls=%fused_computation.5 | loop fusion | flops 2883584 | bytes 10092548 | tf_op jit(solution)/shard_map/convert_element_type | solution.py:322
  9.3 207.6 %shard_map.103 = bf16[1,1,1024,2048]{3,2,1,0:T(8,128)(2,1)} custom-call(bf16[256,2816]{1,0:T(8,128)(2,1)} %get-tuple-element.5.up_delta, bf16[2816,256]{1,0:T(8,128)(2,1)} %get-tuple-element.3.down_delta, bf16[1,1,1,2048,2816]{4,3,2,1,0:T(8,128)(2,1)} %old_up.1, bf16[1,1,1,2816,2048]{4,3,2,1,0:T(8,128)(2,1)} %old_down.1, bf16[1,1,1024,2048]{3,2,1,0:T(8,128)(2,1)} %prompts.1), custom_call_target="tpu_custom_call" | custom-call | tf_op jit(solution)/shard_map/pallas_call | solution.py:325
  216.9 4.8 %copy.13 = bf16[1,1,1024,2048]{3,2,1,0:T(8,128)(2,1)} copy(bf16[1,1,1024,2048]{3,2,1,0:T(8,128)(2,1)} %shard_map.103) | data formatting | bytes 8388608
Async XLA Ops:
  1.3 5.3 %copy-start = (f32[1,1,2816,256]{3,2,1,0:T(8,128)S(1)}, f32[1,1,2816,256]{3,2,1,0:T(8,128)}, u32[]{:S(2)}) copy-start(f32[1,1,2816,256]{3,2,1,0:T(8,128)} %param.9) | copy-start | bytes 8650756
  1.3 5.3 %copy-start.1 = (f32[1,1,2816,256]{3,2,1,0:T(8,128)S(1)}, f32[1,1,2816,256]{3,2,1,0:T(8,128)}, u32[]{:S(2)}) copy-start(f32[1,1,2816,256]{3,2,1,0:T(8,128)} %param.11) | copy-start | bytes 8650756

commit v3 on v2

--- a/solution.py
+++ b/solution.py
@@ -15,16 +15,18 @@
 WHOLE, UPPER, LOWER = (0, 4), (0, 2), (2, 4)
 ARRIVALS = {
     (DX, WHOLE): 0, (DY, WHOLE): 1, (DZ, WHOLE): 2, (DX | DZ, WHOLE): 3, (DY | DZ, WHOLE): 4,
-    (DX | DY, UPPER): 5, (DX | DY, LOWER): 6, (DX | DY | DZ, WHOLE): 7,
+    (DX | DY, UPPER): 5, (DX | DY, LOWER): 6, (DX | DY | DZ, UPPER): 7, (DX | DY | DZ, LOWER): 8,
 }
-HOP1 = ((0, DZ, WHOLE), (0, DX, WHOLE), (0, DY, WHOLE))
+HOP1 = ((0, DX, WHOLE), (0, DY, WHOLE), (0, DZ, WHOLE))
 HOP2 = ((DZ, DX, WHOLE), (DZ, DY, WHOLE), (DY, DX, UPPER), (DX, DY, LOWER))
-HOP3 = ((DX | DY, DZ, WHOLE),)
+HOP3 = ((DX | DY, DZ, UPPER), (DX | DY, DZ, LOWER))
+HOP3_X, HOP3_Y = (DY | DZ, DX, LOWER), (DX | DZ, DY, LOWER)
 SENDS = HOP1 + HOP2 + HOP3
 N_SEMS = len(SENDS) + 2
-WINDOW = 6
+WINDOW = 8
 PACE = 2
-LAST = 4
+EARLY = 10
+LAST = 5
 
 
 def exact_gelu(v):
@@ -146,8 +148,8 @@
             t, yx = place(d)
             return weights.at[c, t, yx, core, pl.ds(blocks[0], blocks[1] - blocks[0])]
 
-        def message(c, i):
-            d, axis, blocks = SENDS[i]
+        def message(c, i, route=None):
+            d, axis, blocks = route or SENDS[i]
             ref = blocks_of(c, d, blocks)
             to = {DX: (side, x_rep), DY: (side, y_rep), DZ: (z_side, rep)}[axis]
             return pltpu.make_async_remote_copy(
@@ -179,13 +181,15 @@
         ping(barrier, z_side, rep)
         ping(barrier, side - 2, rep)
 
-        def clear(i, carry):
-            acc[pl.ds(pl.multiple_of(i * 64, 64), 64), :] = jnp.zeros((64, acc.shape[1]), F32)
+        prompts_in().wait()
+
+        def residual(i, carry):
+            here = pl.ds(pl.multiple_of(i * 64, 64), 64)
+            acc[here, :] = hidden[here, :].astype(F32)
             return carry
 
-        lax.fori_loop(0, tokens // 64, clear, 0)
+        lax.fori_loop(0, tokens // 64, residual, 0)
         pl.semaphore_wait(barrier, 5)
-        prompts_in().wait()
 
         def send_all(c, first, last):
             for i in range(first, last):
@@ -238,44 +242,62 @@
                 pair_message(c, dz, core).wait_send()
 
         def step(i, carry):
-            def during(lag, upto=None):
-                if upto is None:
-                    return pl.when((i >= lag) & (i < n_chunks + lag))
-                return pl.when((i >= lag) & (i < upto + lag))
+            def during(lag):
+                return pl.when((i >= lag) & (i < n_chunks + lag))
 
             @during(0)
             def _():
                 add_own(i)
-                send_all(i, 0, len(HOP1))
+                send_all(i, 0, 3)
+
+            @during(3)
+            def _():
+                c = i - 3
+                arrived(c, DX | DY, UPPER)
+                arrived(c, DX | DY, LOWER)
+                arrived(c, DX | DZ, WHOLE)
+                arrived(c, DY | DZ, WHOLE)
+                message(c, 7).start()
+                early = c < EARLY
+
+                @pl.when(early & (c % 2 == 1))
+                def _():
+                    message(c, 8, HOP3_X).start()
+
+                @pl.when(early & (c % 2 == 0))
+                def _():
+                    message(c, 8, HOP3_Y).start()
+
+                @pl.when(c >= EARLY)
+                def _():
+                    message(c, 8).start()
 
             @during(1)
             def _():
                 arrived(i - 1, DZ, WHOLE)
                 send_all(i - 1, 3, 5)
+
+            @during(3)
+            def _():
+                pair_message(i - 3, 0, core).start()
+
+            @during(LAST)
+            def _():
+                for dz in (0, 1):
+                    pair_message(i - LAST, dz, 1 - core).wait_recv()
+                multiply(i - LAST, 0)
+
+            @during(1)
+            def _():
                 arrived(i - 1, DX, WHOLE)
                 arrived(i - 1, DY, WHOLE)
                 send_all(i - 1, 5, 7)
 
-            @during(LAST)
-            def _():
-                for dz in (0, 1):
-                    pair_message(i - LAST, dz, 1 - core).wait_recv()
-                multiply(i - LAST, 0)
-
-            @during(2)
-            def _():
-                c = i - 2
-                arrived(c, DX | DY, UPPER)
-                arrived(c, DX | DY, LOWER)
-                send_all(c, 7, len(SENDS))
-                pair_message(c, 0, core).start()
-                arrived(c, DX | DZ, WHOLE)
-                arrived(c, DY | DZ, WHOLE)
-
-            @during(3)
-            def _():
-                arrived(i - 3, DX | DY | DZ, WHOLE)
-                pair_message(i - 3, 1, core).start()
+            @during(4)
+            def _():
+                arrived(i - 4, DX | DY | DZ, UPPER)
+                arrived(i - 4, DX | DY | DZ, LOWER)
+                pair_message(i - 4, 1, core).start()
 
             @during(LAST)
             def _():
@@ -299,7 +321,7 @@
 
         def finish(m, carry):
             here = pl.ds(pl.multiple_of(m * finish_rows, finish_rows), finish_rows)
-            hidden[here, :] = (hidden[here, :].astype(F32) + acc[here, :]).astype(BF16)
+            hidden[here, :] = acc[here, :].astype(BF16)
             result_out(m).start()
             return carry
 

time: 223 us -> 211 us (0.946)
  Pallas kernels: 208 us -> 197 us
    pallas_call x1, Pallas kernels: 208 us -> 197 us  [local_step(): pl.pallas_call(functools.partial(sync_kernel, n_chunks), out_shape=jax.Sh...]
where the time goes in v3:
time: 211 us
  Pallas kernels  197 us (93%)
  other arithmetic  8 us (4%)
  local copies, waits for them, and re-layouts  4.8 us (2%)
    pallas_call x1, Pallas kernels, local_step(): pl.pallas_call(functools.partial(sync_kernel, n_chunks), out_shape=jax.Sh...  197 us
    convert_element_type x1, other arithmetic, local_step(): delta_up = (new_up - w_up)[0, 0].astype(BF16)  5.28 us
    unnamed x5, local copies, waits for them, and re-layouts  4.8 us

profile of v3, /device:TPU:24, one launch (start us, length us, event | category | flops | bytes accessed | tf_op | source)
XLA Modules:
  0.0 211.3 jit_solution(92553245927245168)
XLA Ops:
  1.3 0.0 copy-start
  1.3 0.0 copy-start.1
  1.3 5.3 %fusion = (bf16[256,2816]{1,0:T(8,128)(2,1)}, f32[1,1,256,2816]{3,2,1,0:T(8,128)}) fusion(f32[1,1,256,2816]{3,2,1,0:T(8,128)} %param.8, f32[1,1,256,2816]{3,2,1,0:T(8,128)} %param.10, f32[]{:T(128)} %bitcast.5), kind=kLoop, calls=%fused_computation.4 | loop fusion | flops 2883584 | bytes 10092548 | tf_op jit(solution)/shard_map/convert_element_type | solution.py:343
  6.6 0.0 copy-done
  6.6 0.0 copy-done.1
  6.6 2.7 %fusion.1 = (bf16[2816,256]{1,0:T(8,128)(2,1)}, f32[1,1,2816,256]{3,2,1,0:T(8,128)}) fusion(f32[1,1,2816,256]{3,2,1,0:T(8,128)S(1)} %copy-done, f32[1,1,2816,256]{3,2,1,0:T(8,128)S(1)} %copy-done.1, f32[]{:T(128)} %bitcast.6), kind=kLoop, calls=%fused_computation.5 | loop fusion | flops 2883584 | bytes 10092548 | tf_op jit(solution)/shard_map/convert_element_type | solution.py:344
  9.3 197.2 %shard_map.103 = bf16[1,1,1024,2048]{3,2,1,0:T(8,128)(2,1)} custom-call(bf16[256,2816]{1,0:T(8,128)(2,1)} %get-tuple-element.5.up_delta, bf16[2816,256]{1,0:T(8,128)(2,1)} %get-tuple-element.3.down_delta, bf16[1,1,1,2048,2816]{4,3,2,1,0:T(8,128)(2,1)} %old_up.1, bf16[1,1,1,2816,2048]{4,3,2,1,0:T(8,128)(2,1)} %old_down.1, bf16[1,1,1024,2048]{3,2,1,0:T(8,128)(2,1)} %prompts.1), custom_call_target="tpu_custom_call" | custom-call | tf_op jit(solution)/shard_map/pallas_call | solution.py:347
  206.5 4.8 %copy.13 = bf16[1,1,1024,2048]{3,2,1,0:T(8,128)(2,1)} copy(bf16[1,1,1024,2048]{3,2,1,0:T(8,128)(2,1)} %shard_map.103) | data formatting | bytes 8388608
Async XLA Ops:
  1.3 5.3 %copy-start = (f32[1,1,2816,256]{3,2,1,0:T(8,128)S(1)}, f32[1,1,2816,256]{3,2,1,0:T(8,128)}, u32[]{:S(2)}) copy-start(f32[1,1,2816,256]{3,2,1,0:T(8,128)} %param.9) | copy-start | bytes 8650756
  1.3 5.3 %copy-start.1 = (f32[1,1,2816,256]{3,2,1,0:T(8,128)S(1)}, f32[1,1,2816,256]{3,2,1,0:T(8,128)}, u32[]{:S(2)}) copy-start(f32[1,1,2816,256]{3,2,1,0:T(8,128)} %param.11) | copy-start | bytes 8650756

commit v4 on v3

--- a/solution.py
+++ b/solution.py
@@ -27,6 +27,7 @@
 PACE = 2
 EARLY = 10
 LAST = 5
+VMEM_BYTES = 58 * 2**20
 
 
 def exact_gelu(v):
@@ -34,9 +35,9 @@
 
 
 def sync_kernel(
-    n_chunks, up_delta, down_delta, old_up, old_down, prompts, y_ref,
-    weights, acc, hidden, stale,
-    own_recv, send_sem, recv_sem, pair_recv, stale_sem, io_sem, pace_sem, credit_sem,
+    n_chunks, learn_rate, w_up, w_down, g_up, g_down, old_up, old_down, prompts, zeroed_up, zeroed_down, hidden,
+    weights, acc, stale, up_pair, down_pair,
+    own_recv, send_sem, recv_sem, pair_recv, stale_sem, fetch_sem, io_sem, pace_sem, credit_sem,
 ):
     side = lax.axis_index("side")
     rep = lax.axis_index("rep")
@@ -46,6 +47,7 @@
     rank = side % 2
     tokens = hidden.shape[0]
     rows = 2 * LANES
+    del zeroed_up, zeroed_down
 
     barrier = pltpu.get_barrier_semaphore()
 
@@ -61,32 +63,55 @@
         return pl.ds(pl.multiple_of(c * LANES, LANES), LANES)
 
     def prompts_in():
-        return pltpu.make_async_copy(prompts.at[0, 0], hidden, io_sem.at[0])
+        return pltpu.make_async_copy(prompts.at[0, 0], hidden, io_sem)
 
     @pl.when(side < 2)
     def _():
-        def delta_copies(c):
+        def fetches(c):
+            slot = c % 2
+            return [
+                pltpu.make_async_copy(src, dst, fetch_sem.at[slot, i])
+                for i, (src, dst) in enumerate(
+                    (
+                        (w_up.at[0, 0, :, columns(c)], up_pair.at[slot, 0]),
+                        (g_up.at[0, 0, :, columns(c)], up_pair.at[slot, 1]),
+                        (w_down.at[0, 0, columns(c), :], down_pair.at[slot, 0]),
+                        (g_down.at[0, 0, columns(c), :], down_pair.at[slot, 1]),
+                    )
+                )
+            ]
+
+        def fetch(c):
+            for copy in fetches(c):
+                copy.start()
+
+        def prepare(c):
+            for copy in fetches(c):
+                copy.wait()
+            rate = learn_rate[0]
             slot = weights.at[c, rank, rep // 2, core]
-
-            def copy(src, dst, i):
-                return pltpu.make_async_remote_copy(
-                    src_ref=src, dst_ref=dst, send_sem=send_sem.at[c % WINDOW, i], recv_sem=own_recv.at[c, i],
-                    device_id=(side + 2, rep), device_id_type=MESH,
-                )
-
-            return (
-                [copy(up_delta.at[pl.ds(i * LANES, LANES), columns(c)], slot.at[i], i) for i in (0, 1)]
-                + [copy(down_delta.at[columns(c), pl.ds(i * LANES, LANES)], slot.at[2 + i], 2 + i) for i in (0, 1)]
+            for i in (0, 1):
+                part = slice(i * LANES, (i + 1) * LANES)
+                for j, pair, here in ((0, up_pair, (part, slice(None))), (2, down_pair, (slice(None), part))):
+                    old = pair[(c % 2, 0) + here]
+                    slot[j + i] = ((old - rate * pair[(c % 2, 1) + here]) - old).astype(BF16)
+
+        def delta_copy(c):
+            ref = weights.at[c, rank, rep // 2, core]
+            return pltpu.make_async_remote_copy(
+                src_ref=ref, dst_ref=ref, send_sem=send_sem.at[c % WINDOW, 0], recv_sem=own_recv.at[c],
+                device_id=(side + 2, rep), device_id_type=MESH,
             )
 
+        fetch(0)
+        fetch(1)
         prompts_in().start()
         ping(barrier, side + 2, rep)
         ping(barrier, 1 - side, rep)
+        for c in (0, 1):
+            prepare(c)
+            fetch(c + 2)
         pl.semaphore_wait(barrier, 2)
-
-        def sent(c):
-            for copy in delta_copies(c):
-                copy.wait_send()
 
         def send(c, carry):
             @pl.when(c >= PACE)
@@ -97,12 +122,19 @@
             def _():
                 pl.semaphore_wait(pace_sem, 1)
 
-            for copy in delta_copies(c):
-                copy.start()
+            delta_copy(c).start()
+
+            @pl.when(c + 2 < n_chunks)
+            def _():
+                prepare(c + 2)
+
+            @pl.when(c + 4 < n_chunks)
+            def _():
+                fetch(c + 4)
 
             @pl.when(c >= 1)
             def _():
-                sent(c - 1)
+                delta_copy(c - 1).wait_send()
 
             @pl.when((side == 1) & (c >= 1))
             def _():
@@ -111,11 +143,8 @@
             return carry
 
         lax.fori_loop(0, n_chunks, send, 0)
-        sent(n_chunks - 1)
+        delta_copy(n_chunks - 1).wait_send()
         prompts_in().wait()
-        out = pltpu.make_async_copy(hidden, y_ref.at[0, 0], io_sem.at[1])
-        out.start()
-        out.wait()
 
     @pl.when(side >= 2)
     def _():
@@ -197,11 +226,10 @@
 
         def add_own(c):
             slot = weights.at[c, rank, rep // 2, core]
-            for i in range(4):
-                pltpu.make_async_remote_copy(
-                    src_ref=slot.at[i], dst_ref=slot.at[i], send_sem=send_sem.at[0, 0], recv_sem=own_recv.at[c, i],
-                    device_id=(side - 2, rep), device_id_type=MESH,
-                ).wait_recv()
+            pltpu.make_async_remote_copy(
+                src_ref=slot, dst_ref=slot, send_sem=send_sem.at[0, 0], recv_sem=own_recv.at[c],
+                device_id=(side - 2, rep), device_id_type=MESH,
+            ).wait_recv()
             for copy in stale_copies(c):
                 copy.wait()
             for i in range(4):
@@ -313,21 +341,51 @@
         for c in range(n_chunks + LAST - (WINDOW - 1), n_chunks):
             drain(c)
 
-        finish_rows = tokens // 4
-
-        def result_out(m):
-            here = pl.ds(pl.multiple_of(m * finish_rows, finish_rows), finish_rows)
-            return pltpu.make_async_copy(hidden.at[here, :], y_ref.at[0, 0, here, :], io_sem.at[m])
-
-        def finish(m, carry):
-            here = pl.ds(pl.multiple_of(m * finish_rows, finish_rows), finish_rows)
+        def finish(i, carry):
+            here = pl.ds(pl.multiple_of(i * 64, 64), 64)
             hidden[here, :] = acc[here, :].astype(BF16)
-            result_out(m).start()
             return carry
 
-        lax.fori_loop(0, 4, finish, 0)
-        for m in range(4):
-            result_out(m).wait()
+        lax.fori_loop(0, tokens // 64, finish, 0)
+
+
+def zero_kernel(up_ref, down_ref, zeros, sems):
+    @pl.when(lax.axis_index("side") >= 2)
+    def _():
+        zeros[...] = jnp.zeros_like(zeros)
+        copies = []
+        for n, ref in enumerate((up_ref.at[0, 0], down_ref.at[0, 0])):
+            high, wide = ref.shape
+            for i in range(high // zeros.shape[0]):
+                for j in range(wide // zeros.shape[1]):
+                    part = ref.at[pl.ds(i * zeros.shape[0], zeros.shape[0]), pl.ds(j * zeros.shape[1], zeros.shape[1])]
+                    copies.append(pltpu.make_async_copy(zeros, part, sems.at[n]))
+        for copy in copies:
+            copy.start()
+        for copy in copies:
+            copy.wait()
+
+
+def last_kernel(learn_rate, w_up, w_down, g_up, g_down, up_in, down_in, hidden, up_out, down_out, y_ref, sem):
+    del up_in, down_in
+    result = pltpu.make_async_copy(hidden, y_ref.at[0, 0], sem)
+    result.start()
+
+    @pl.when(lax.axis_index("side") < 2)
+    def _():
+        rate = learn_rate[0]
+
+        def body(w, g, out):
+            out[...] = w[...] - rate * g[...]
+
+        for w, g, out in ((w_up, g_up, up_out), (w_down, g_down, down_out)):
+            high, wide = w.shape[2:]
+            spec = pl.BlockSpec((high // 8, wide), lambda i: (i, 0))
+            pltpu.emit_pipeline(body, grid=(8,), in_specs=[spec, spec], out_specs=[spec])(
+                w.at[0, 0], g.at[0, 0], out.at[0, 0]
+            )
+
+    result.wait()
 
 
 def solution(mesh):
@@ -337,37 +395,57 @@
     token_spec = P("side", "rep", None, None)
 
     def local_step(w_up, w_down, g_up, g_down, learn_rate, old_up, old_down, prompts):
-        step_rate = learn_rate[0]
-        new_up = w_up - step_rate * g_up
-        new_down = w_down - step_rate * g_down
-        delta_up = (new_up - w_up)[0, 0].astype(BF16)
-        delta_down = (new_down - w_down)[0, 0].astype(BF16)
-        n_chunks = delta_up.shape[1] // LANES
+        n_chunks = w_up.shape[3] // LANES
         tokens, model = prompts.shape[2:]
-        y = pl.pallas_call(
+        rows = w_up.shape[2]
+        anywhere = pl.BlockSpec(memory_space=pl.ANY)
+        scalar = pl.BlockSpec(memory_space=pltpu.SMEM)
+        on_chip = pl.BlockSpec(memory_space=pltpu.VMEM)
+        new_shapes = [jax.ShapeDtypeStruct(w.shape, F32) for w in (w_up, w_down)]
+        zero_up, zero_down = pl.pallas_call(
+            zero_kernel,
+            out_shape=new_shapes,
+            out_specs=[anywhere] * 2,
+            scratch_shapes=[pltpu.VMEM((256, 256), F32), pltpu.SemaphoreType.DMA((2,))],
+            compiler_params=pltpu.CompilerParams(has_side_effects=True, vmem_limit_bytes=32 * 2**20),
+        )()
+        hidden = pl.pallas_call(
             functools.partial(sync_kernel, n_chunks),
-            out_shape=jax.ShapeDtypeStruct(prompts.shape, BF16),
-            in_specs=[pl.BlockSpec(memory_space=pl.ANY)] * 5,
-            out_specs=pl.BlockSpec(memory_space=pl.ANY),
+            out_shape=pltpu.VMEM((tokens, model), BF16),
+            in_specs=[scalar] + [anywhere] * 9,
+            out_specs=on_chip,
             scratch_shapes=[
                 pltpu.VMEM((n_chunks, 2, 4, 2, 4, LANES, LANES), BF16),
                 pltpu.VMEM((tokens, model), F32),
-                pltpu.VMEM((tokens, model), BF16),
                 pltpu.VMEM((2, 4, LANES, LANES), BF16),
-                pltpu.SemaphoreType.DMA((n_chunks, 4)),
+                pltpu.VMEM((2, 2, rows, LANES), F32),
+                pltpu.VMEM((2, 2, LANES, rows), F32),
+                pltpu.SemaphoreType.DMA((n_chunks,)),
                 pltpu.SemaphoreType.DMA((WINDOW, N_SEMS)),
                 pltpu.SemaphoreType.DMA((n_chunks, len(ARRIVALS))),
                 pltpu.SemaphoreType.DMA((n_chunks, 2)),
                 pltpu.SemaphoreType.DMA((2, 4)),
-                pltpu.SemaphoreType.DMA((4,)),
+                pltpu.SemaphoreType.DMA((2, 4)),
+                pltpu.SemaphoreType.DMA,
                 pltpu.SemaphoreType.REGULAR,
                 pltpu.SemaphoreType.REGULAR,
             ],
             compiler_params=pltpu.CompilerParams(
-                collective_id=0, has_side_effects=True, vmem_limit_bytes=67043328
+                collective_id=0, has_side_effects=True, vmem_limit_bytes=VMEM_BYTES
             ),
-        )(delta_up, delta_down, old_up, old_down, prompts)
-        return new_up, new_down, y
+        )(learn_rate, w_up, w_down, g_up, g_down, old_up, old_down, prompts, zero_up, zero_down)
+        return pl.pallas_call(
+            last_kernel,
+            out_shape=new_shapes + [jax.ShapeDtypeStruct(prompts.shape, BF16)],
+            in_specs=[scalar] + [anywhere] * 6 + [on_chip],
+            out_specs=[anywhere] * 3,
+            input_output_aliases={5: 0, 6: 1},
+            scratch_shapes=[pltpu.SemaphoreType.DMA],
+            compiler_params=pltpu.CompilerParams(vmem_limit_bytes=VMEM_BYTES),
+        )(
+            learn_rate, w_up, w_down, g_up, g_down, zero_up, zero_down,
+            pltpu.with_memory_space_constraint(hidden, pltpu.VMEM),
+        )
 
     return jax.shard_map(
         local_step,

time: 211 us -> 201 us (0.953)
  other arithmetic: 8 us -> 0 us
  local copies, waits for them, and re-layouts: 4.8 us -> 0 us
  Pallas kernels: 197 us -> 200 us
    convert_element_type x2 -> x0, other arithmetic: 8 us -> none  [the longest x1 5.28 us: local_step(): delta_up = (new_up - w_up)[0, 0].astype(BF16)]
    unnamed x5 -> x0, local copies, waits for them, and re-layouts: 4.8 us -> none
    pallas_call x1 -> x3, Pallas kernels: 197 us -> 200 us  [the longest x1 195 us: local_step(): pl.pallas_call(functools.partial(sync_kernel, n_chunks), out_shape=pltpu....]
where the time goes in v4:
time: 201 us
  Pallas kernels  200 us (100%)
    pallas_call x1, Pallas kernels, local_step(): pl.pallas_call(functools.partial(sync_kernel, n_chunks), out_shape=pltpu....  195 us

profile of v4, /device:TPU:24, one launch (start us, length us, event | category | flops | bytes accessed | tf_op | source)
XLA Modules:
  0.0 200.9 jit_solution(14344167731649694590)
XLA Ops:
  1.3 2.5 %shard_map.103 = (f32[1,1,256,2816]{3,2,1,0:T(8,128)}, f32[1,1,2816,256]{3,2,1,0:T(8,128)}) custom-call(), custom_call_target="tpu_custom_call" | custom-call | tf_op jit(solution)/shard_map/pallas_call | solution.py:405
  3.8 195.1 %shard_map.104.hidden = bf16[1024,2048]{1,0:T(8,128)(2,1)S(1)} custom-call(f32[1]{0:T(128)S(6)} %copy.15.learn_rate, f32[1,1,256,2816]{3,2,1,0:T(8,128)} %w_up.3, f32[1,1,2816,256]{3,2,1,0:T(8,128)} %w_down.3, f32[1,1,256,2816]{3,2,1,0:T(8,128)} %g_up.3, f32[1,1,2816,256]{3,2,1,0:T(8,128)} %g_down.3, bf16[1,1,1,2048,2816]{4,3,2,1,0:T(8,128)(2,1)} %old_up.1, ...), custom_call_target="tpu_custom_call" | custom-call | tf_op jit(solution)/shard_map/pallas_call | solution.py:412
  198.9 2.0 %shard_map.105 = (f32[1,1,256,2816]{3,2,1,0:T(8,128)}, f32[1,1,2816,256]{3,2,1,0:T(8,128)}, bf16[1,1,1024,2048]{3,2,1,0:T(8,128)(2,1)}) custom-call(f32[1]{0:T(128)S(6)} %copy.15.learn_rate, f32[1,1,256,2816]{3,2,1,0:T(8,128)} %w_up.3, f32[1,1,2816,256]{3,2,1,0:T(8,128)} %w_down.3, ...), custom_call_target="tpu_custom_call", output_to_operand_aliasing={{0}: (5, {}), {1}: (6, {})} | custom-call | tf_op jit(solution)/shard_map/pallas_call | solution.py:437

commit v5 on v4

--- a/solution.py
+++ b/solution.py
@@ -27,7 +27,8 @@
 PACE = 2
 EARLY = 10
 LAST = 5
-VMEM_BYTES = 58 * 2**20
+VMEM_BYTES = 54 * 2**20
+FINISH = 64
 
 
 def exact_gelu(v):
@@ -35,8 +36,8 @@
 
 
 def sync_kernel(
-    n_chunks, learn_rate, w_up, w_down, g_up, g_down, old_up, old_down, prompts, zeroed_up, zeroed_down, hidden,
-    weights, acc, stale, up_pair, down_pair,
+    n_chunks, learn_rate, w_up, w_down, g_up, g_down, old_up, old_down, prompts, acc,
+    weights, hidden, stale, up_pair, down_pair,
     own_recv, send_sem, recv_sem, pair_recv, stale_sem, fetch_sem, io_sem, pace_sem, credit_sem,
 ):
     side = lax.axis_index("side")
@@ -47,7 +48,6 @@
     rank = side % 2
     tokens = hidden.shape[0]
     rows = 2 * LANES
-    del zeroed_up, zeroed_down
 
     barrier = pltpu.get_barrier_semaphore()
 
@@ -64,6 +64,11 @@
 
     def prompts_in():
         return pltpu.make_async_copy(prompts.at[0, 0], hidden, io_sem)
+
+    def residual(i, carry):
+        here = pl.ds(pl.multiple_of(i * 64, 64), 64)
+        acc[here, :] = hidden[here, :].astype(F32)
+        return carry
 
     @pl.when(side < 2)
     def _():
@@ -145,6 +150,7 @@
         lax.fori_loop(0, n_chunks, send, 0)
         delta_copy(n_chunks - 1).wait_send()
         prompts_in().wait()
+        lax.fori_loop(0, tokens // 64, residual, 0)
 
     @pl.when(side >= 2)
     def _():
@@ -211,12 +217,6 @@
         ping(barrier, side - 2, rep)
 
         prompts_in().wait()
-
-        def residual(i, carry):
-            here = pl.ds(pl.multiple_of(i * 64, 64), 64)
-            acc[here, :] = hidden[here, :].astype(F32)
-            return carry
-
         lax.fori_loop(0, tokens // 64, residual, 0)
         pl.semaphore_wait(barrier, 5)
 
@@ -341,51 +341,59 @@
         for c in range(n_chunks + LAST - (WINDOW - 1), n_chunks):
             drain(c)
 
-        def finish(i, carry):
-            here = pl.ds(pl.multiple_of(i * 64, 64), 64)
-            hidden[here, :] = acc[here, :].astype(BF16)
-            return carry
-
-        lax.fori_loop(0, tokens // 64, finish, 0)
-
-
-def zero_kernel(up_ref, down_ref, zeros, sems):
-    @pl.when(lax.axis_index("side") >= 2)
-    def _():
-        zeros[...] = jnp.zeros_like(zeros)
-        copies = []
-        for n, ref in enumerate((up_ref.at[0, 0], down_ref.at[0, 0])):
+
+def last_kernel(learn_rate, w_up, w_down, g_up, g_down, acc, up_out, down_out, y_ref, result, zeros, sem, zero_sem):
+    tokens = result.shape[0]
+    is_gen = lax.axis_index("side") >= 2
+    blocks = tokens // FINISH
+
+    def zero_copies():
+        for ref in (up_out.at[0, 0], down_out.at[0, 0]):
             high, wide = ref.shape
             for i in range(high // zeros.shape[0]):
                 for j in range(wide // zeros.shape[1]):
                     part = ref.at[pl.ds(i * zeros.shape[0], zeros.shape[0]), pl.ds(j * zeros.shape[1], zeros.shape[1])]
-                    copies.append(pltpu.make_async_copy(zeros, part, sems.at[n]))
-        for copy in copies:
+                    yield pltpu.make_async_copy(zeros, part, zero_sem)
+
+    @pl.when(is_gen)
+    def _():
+        zeros[...] = jnp.zeros_like(zeros)
+        for copy in zero_copies():
             copy.start()
-        for copy in copies:
+
+    def out(m):
+        here = pl.ds(pl.multiple_of(m * FINISH, FINISH), FINISH)
+        return pltpu.make_async_copy(result.at[here, :], y_ref.at[0, 0, here, :], sem)
+
+    def finish(m, carry):
+        here = pl.ds(pl.multiple_of(m * FINISH, FINISH), FINISH)
+        result[here, :] = acc[here, :].astype(BF16)
+        out(m).start()
+        return carry
+
+    lax.fori_loop(0, blocks, finish, 0)
+
+    @pl.when(is_gen)
+    def _():
+        for copy in zero_copies():
             copy.wait()
 
-
-def last_kernel(learn_rate, w_up, w_down, g_up, g_down, up_in, down_in, hidden, up_out, down_out, y_ref, sem):
-    del up_in, down_in
-    result = pltpu.make_async_copy(hidden, y_ref.at[0, 0], sem)
-    result.start()
-
-    @pl.when(lax.axis_index("side") < 2)
+    @pl.when(jnp.logical_not(is_gen))
     def _():
         rate = learn_rate[0]
 
-        def body(w, g, out):
-            out[...] = w[...] - rate * g[...]
-
-        for w, g, out in ((w_up, g_up, up_out), (w_down, g_down, down_out)):
+        def body(w, g, new):
+            new[...] = w[...] - rate * g[...]
+
+        for w, g, new in ((w_up, g_up, up_out), (w_down, g_down, down_out)):
             high, wide = w.shape[2:]
             spec = pl.BlockSpec((high // 8, wide), lambda i: (i, 0))
             pltpu.emit_pipeline(body, grid=(8,), in_specs=[spec, spec], out_specs=[spec])(
-                w.at[0, 0], g.at[0, 0], out.at[0, 0]
+                w.at[0, 0], g.at[0, 0], new.at[0, 0]
             )
 
-    result.wait()
+    for m in range(blocks):
+        out(m).wait()
 
 
 def solution(mesh):
@@ -402,21 +410,14 @@
         scalar = pl.BlockSpec(memory_space=pltpu.SMEM)
         on_chip = pl.BlockSpec(memory_space=pltpu.VMEM)
         new_shapes = [jax.ShapeDtypeStruct(w.shape, F32) for w in (w_up, w_down)]
-        zero_up, zero_down = pl.pallas_call(
-            zero_kernel,
-            out_shape=new_shapes,
-            out_specs=[anywhere] * 2,
-            scratch_shapes=[pltpu.VMEM((256, 256), F32), pltpu.SemaphoreType.DMA((2,))],
-            compiler_params=pltpu.CompilerParams(has_side_effects=True, vmem_limit_bytes=32 * 2**20),
-        )()
-        hidden = pl.pallas_call(
+        total = pl.pallas_call(
             functools.partial(sync_kernel, n_chunks),
-            out_shape=pltpu.VMEM((tokens, model), BF16),
-            in_specs=[scalar] + [anywhere] * 9,
+            out_shape=pltpu.VMEM((tokens, model), F32),
+            in_specs=[scalar] + [anywhere] * 7,
             out_specs=on_chip,
             scratch_shapes=[
                 pltpu.VMEM((n_chunks, 2, 4, 2, 4, LANES, LANES), BF16),
-                pltpu.VMEM((tokens, model), F32),
+                pltpu.VMEM((tokens, model), BF16),
                 pltpu.VMEM((2, 4, LANES, LANES), BF16),
                 pltpu.VMEM((2, 2, rows, LANES), F32),
                 pltpu.VMEM((2, 2, LANES, rows), F32),
@@ -433,19 +434,20 @@
             compiler_params=pltpu.CompilerParams(
                 collective_id=0, has_side_effects=True, vmem_limit_bytes=VMEM_BYTES
             ),
-        )(learn_rate, w_up, w_down, g_up, g_down, old_up, old_down, prompts, zero_up, zero_down)
+        )(learn_rate, w_up, w_down, g_up, g_down, old_up, old_down, prompts)
         return pl.pallas_call(
             last_kernel,
             out_shape=new_shapes + [jax.ShapeDtypeStruct(prompts.shape, BF16)],
-            in_specs=[scalar] + [anywhere] * 6 + [on_chip],
+            in_specs=[scalar] + [anywhere] * 4 + [on_chip],
             out_specs=[anywhere] * 3,
-            input_output_aliases={5: 0, 6: 1},
-            scratch_shapes=[pltpu.SemaphoreType.DMA],
+            scratch_shapes=[
+                pltpu.VMEM((tokens, model), BF16),
+                pltpu.VMEM((256, 256), F32),
+                pltpu.SemaphoreType.DMA,
+                pltpu.SemaphoreType.DMA,
+            ],
             compiler_params=pltpu.CompilerParams(vmem_limit_bytes=VMEM_BYTES),
-        )(
-            learn_rate, w_up, w_down, g_up, g_down, zero_up, zero_down,
-            pltpu.with_memory_space_constraint(hidden, pltpu.VMEM),
-        )
+        )(learn_rate, w_up, w_down, g_up, g_down, pltpu.with_memory_space_constraint(total, pltpu.VMEM))
 
     return jax.shard_map(
         local_step,

time: 201 us -> 200 us (level)
    pallas_call x1 -> x0, Pallas kernels: 2.51 us -> none  [local_step(): pl.pallas_call(zero_kernel, out_shape=new_shapes, out_specs=[anywhere] *...]
where the time goes in v5:
time: 200 us
  Pallas kernels  198 us (99%)
    pallas_call x1, Pallas kernels, local_step(): pl.pallas_call(functools.partial(sync_kernel, n_chunks), out_shape=pltpu....  195 us

profile of v5, /device:TPU:24, one launch (start us, length us, event | category | flops | bytes accessed | tf_op | source)
XLA Modules:
  0.0 199.7 jit_solution(10302150224027971444)
XLA Ops:
  1.3 194.6 %shard_map.103.acc = f32[1024,2048]{1,0:T(8,128)S(1)} custom-call(f32[1]{0:T(128)S(6)} %copy.11.learn_rate, f32[1,1,256,2816]{3,2,1,0:T(8,128)} %w_up.3, f32[1,1,2816,256]{3,2,1,0:T(8,128)} %w_down.3, f32[1,1,256,2816]{3,2,1,0:T(8,128)} %g_up.3, f32[1,1,2816,256]{3,2,1,0:T(8,128)} %g_down.3, bf16[1,1,1,2048,2816]{4,3,2,1,0:T(8,128)(2,1)} %old_up.1, ...), custom_call_target="tpu_custom_call" | custom-call | tf_op jit(solution)/shard_map/pallas_call | solution.py:413
  195.9 3.8 %shard_map.104 = (f32[1,1,256,2816]{3,2,1,0:T(8,128)}, f32[1,1,2816,256]{3,2,1,0:T(8,128)}, bf16[1,1,1024,2048]{3,2,1,0:T(8,128)(2,1)}) custom-call(f32[1]{0:T(128)S(6)} %copy.11.learn_rate, f32[1,1,256,2816]{3,2,1,0:T(8,128)} %w_up.3, f32[1,1,2816,256]{3,2,1,0:T(8,128)} %w_down.3, f32[1,1,256,2816]{3,2,1,0:T(8,128)} %g_up.3, f32[1,1,2816,256]{3,2,1,0:T(8,128)} %g_down.3, ...), custom_call_target="tpu_custom_call" | custom-call | tf_op jit(solution)/shard_map/pallas_call | solution.py:438

commit v6 on v5

--- a/solution.py
+++ b/solution.py
@@ -12,7 +12,7 @@
 BF16 = jnp.bfloat16
 LANES = 128
 DX, DY, DZ = 1, 2, 4
-WHOLE, UPPER, LOWER = (0, 4), (0, 2), (2, 4)
+WHOLE, UPPER, LOWER = (0, 2), (0, 1), (1, 2)
 ARRIVALS = {
     (DX, WHOLE): 0, (DY, WHOLE): 1, (DZ, WHOLE): 2, (DX | DZ, WHOLE): 3, (DY | DZ, WHOLE): 4,
     (DX | DY, UPPER): 5, (DX | DY, LOWER): 6, (DX | DY | DZ, UPPER): 7, (DX | DY | DZ, LOWER): 8,
@@ -23,10 +23,10 @@
 HOP3_X, HOP3_Y = (DY | DZ, DX, LOWER), (DX | DZ, DY, LOWER)
 SENDS = HOP1 + HOP2 + HOP3
 N_SEMS = len(SENDS) + 2
-WINDOW = 8
-PACE = 2
-EARLY = 10
-LAST = 5
+WINDOW = 10
+PACE = 3
+EARLY = 28
+LAST = 9
 VMEM_BYTES = 54 * 2**20
 FINISH = 64
 
@@ -48,6 +48,7 @@
     rank = side % 2
     tokens = hidden.shape[0]
     rows = 2 * LANES
+    n_parts = 2 * n_chunks
 
     barrier = pltpu.get_barrier_semaphore()
 
@@ -101,10 +102,10 @@
                     old = pair[(c % 2, 0) + here]
                     slot[j + i] = ((old - rate * pair[(c % 2, 1) + here]) - old).astype(BF16)
 
-        def delta_copy(c):
-            ref = weights.at[c, rank, rep // 2, core]
+        def delta_copy(s):
+            ref = weights.at[s // 2, rank, rep // 2, core, pl.ds(2 * (s % 2), 2)]
             return pltpu.make_async_remote_copy(
-                src_ref=ref, dst_ref=ref, send_sem=send_sem.at[c % WINDOW, 0], recv_sem=own_recv.at[c],
+                src_ref=ref, dst_ref=ref, send_sem=send_sem.at[s % WINDOW, 0], recv_sem=own_recv.at[s],
                 device_id=(side + 2, rep), device_id_type=MESH,
             )
 
@@ -113,42 +114,40 @@
         prompts_in().start()
         ping(barrier, side + 2, rep)
         ping(barrier, 1 - side, rep)
-        for c in (0, 1):
-            prepare(c)
-            fetch(c + 2)
+        prepare(0)
         pl.semaphore_wait(barrier, 2)
 
-        def send(c, carry):
-            @pl.when(c >= PACE)
+        def send(s, carry):
+            @pl.when(s >= PACE)
             def _():
                 pl.semaphore_wait(credit_sem, 1)
 
-            @pl.when((side == 0) & (c >= 1))
+            @pl.when((side == 0) & (s >= 1))
             def _():
                 pl.semaphore_wait(pace_sem, 1)
 
-            delta_copy(c).start()
-
-            @pl.when(c + 2 < n_chunks)
-            def _():
-                prepare(c + 2)
-
-            @pl.when(c + 4 < n_chunks)
-            def _():
-                fetch(c + 4)
-
-            @pl.when(c >= 1)
-            def _():
-                delta_copy(c - 1).wait_send()
-
-            @pl.when((side == 1) & (c >= 1))
+            delta_copy(s).start()
+
+            @pl.when((s % 2 == 0) & (s // 2 + 2 < n_chunks))
+            def _():
+                fetch(s // 2 + 2)
+
+            @pl.when((s % 2 == 0) & (s // 2 + 1 < n_chunks))
+            def _():
+                prepare(s // 2 + 1)
+
+            @pl.when(s >= 1)
+            def _():
+                delta_copy(s - 1).wait_send()
+
+            @pl.when((side == 1) & (s >= 1))
             def _():
                 ping(pace_sem, 0, rep)
 
             return carry
 
-        lax.fori_loop(0, n_chunks, send, 0)
-        delta_copy(n_chunks - 1).wait_send()
+        lax.fori_loop(0, n_parts, send, 0)
+        delta_copy(n_parts - 1).wait_send()
         prompts_in().wait()
         lax.fori_loop(0, tokens // 64, residual, 0)
 
@@ -181,7 +180,7 @@
 
         def blocks_of(c, d, blocks):
             t, yx = place(d)
-            return weights.at[c, t, yx, core, pl.ds(blocks[0], blocks[1] - blocks[0])]
+            return weights.at[c // 2, t, yx, core, pl.ds(2 * (c % 2) + blocks[0], blocks[1] - blocks[0])]
 
         def message(c, i, route=None):
             d, axis, blocks = route or SENDS[i]
@@ -201,7 +200,7 @@
 
         def pair_message(c, dz, of_core):
             t = 1 - rank if dz else rank
-            ref = weights.at[c, t, :, of_core]
+            ref = weights.at[c // 2, t, :, of_core, pl.ds(2 * (c % 2), 2)]
             return pltpu.make_async_remote_copy(
                 src_ref=ref, dst_ref=ref, send_sem=send_sem.at[c % WINDOW, len(SENDS) + dz],
                 recv_sem=pair_recv.at[c, dz], device_id=(side, pair_rep), device_id_type=MESH,
@@ -224,22 +223,29 @@
             for i in range(first, last):
                 message(c, i).start()
 
-        def add_own(c):
+        def add_own(s):
+            c, h = s // 2, s % 2
             slot = weights.at[c, rank, rep // 2, core]
+            part = slot.at[pl.ds(2 * h, 2)]
             pltpu.make_async_remote_copy(
-                src_ref=slot, dst_ref=slot, send_sem=send_sem.at[0, 0], recv_sem=own_recv.at[c],
+                src_ref=part, dst_ref=part, send_sem=send_sem.at[0, 0], recv_sem=own_recv.at[s],
                 device_id=(side - 2, rep), device_id_type=MESH,
             ).wait_recv()
-            for copy in stale_copies(c):
-                copy.wait()
-            for i in range(4):
-                slot[i] = (stale[c % 2, i].astype(F32) + slot[i].astype(F32)).astype(BF16)
-
-            @pl.when(c + PACE < n_chunks)
+
+            @pl.when(h == 0)
+            def _():
+                for copy in stale_copies(c):
+                    copy.wait()
+
+            for i in (0, 1):
+                new = stale[c % 2, 2 * h + i].astype(F32) + slot[2 * h + i].astype(F32)
+                slot[2 * h + i] = new.astype(BF16)
+
+            @pl.when(s + PACE < n_parts)
             def _():
                 ping(credit_sem, side - 2, rep)
 
-            @pl.when(c + 2 < n_chunks)
+            @pl.when((h == 1) & (c + 2 < n_chunks))
             def _():
                 for copy in stale_copies(c + 2):
                     copy.start()
@@ -247,7 +253,7 @@
         half = tokens // 2
 
         def multiply(c, m):
-            here = slice(m * half, (m + 1) * half)
+            here = pl.ds(pl.multiple_of(m * half, half), half)
             up_mat = jnp.concatenate(
                 [weights[c, t, :, :, 0:2].reshape(acc.shape[1], LANES) for t in (0, 1)], axis=1
             )
@@ -271,75 +277,74 @@
 
         def step(i, carry):
             def during(lag):
-                return pl.when((i >= lag) & (i < n_chunks + lag))
+                return pl.when((i >= lag) & (i < n_parts + lag))
+
+            @during(LAST)
+            def _():
+                s = i - LAST
+
+                @pl.when(s % 2 == 0)
+                def _():
+                    for part in (0, 1):
+                        for dz in (0, 1):
+                            pair_message(s + part, dz, 1 - core).wait_recv()
+
+                multiply(s // 2, s % 2)
+
+            @during(2)
+            def _():
+                arrived(i - 2, DX, WHOLE)
+                arrived(i - 2, DY, WHOLE)
+                send_all(i - 2, 5, 7)
 
             @during(0)
             def _():
                 add_own(i)
                 send_all(i, 0, 3)
 
-            @during(3)
-            def _():
-                c = i - 3
-                arrived(c, DX | DY, UPPER)
-                arrived(c, DX | DY, LOWER)
-                arrived(c, DX | DZ, WHOLE)
-                arrived(c, DY | DZ, WHOLE)
-                message(c, 7).start()
-                early = c < EARLY
-
-                @pl.when(early & (c % 2 == 1))
+            @during(2)
+            def _():
+                arrived(i - 2, DZ, WHOLE)
+                send_all(i - 2, 3, 5)
+
+            @during(4)
+            def _():
+                s = i - 4
+                arrived(s, DX | DY, UPPER)
+                arrived(s, DX | DY, LOWER)
+                arrived(s, DX | DZ, WHOLE)
+                arrived(s, DY | DZ, WHOLE)
+                message(s, 7).start()
+                early = s < EARLY
+                odd = s // 2 % 2 == 1
+
+                @pl.when(early & odd)
                 def _():
-                    message(c, 8, HOP3_X).start()
-
-                @pl.when(early & (c % 2 == 0))
+                    message(s, 8, HOP3_X).start()
+
+                @pl.when(early & jnp.logical_not(odd))
                 def _():
-                    message(c, 8, HOP3_Y).start()
-
-                @pl.when(c >= EARLY)
+                    message(s, 8, HOP3_Y).start()
+
+                @pl.when(s >= EARLY)
                 def _():
-                    message(c, 8).start()
-
-            @during(1)
-            def _():
-                arrived(i - 1, DZ, WHOLE)
-                send_all(i - 1, 3, 5)
-
-            @during(3)
-            def _():
-                pair_message(i - 3, 0, core).start()
-
-            @during(LAST)
-            def _():
-                for dz in (0, 1):
-                    pair_message(i - LAST, dz, 1 - core).wait_recv()
-                multiply(i - LAST, 0)
-
-            @during(1)
-            def _():
-                arrived(i - 1, DX, WHOLE)
-                arrived(i - 1, DY, WHOLE)
-                send_all(i - 1, 5, 7)
-
-            @during(4)
-            def _():
-                arrived(i - 4, DX | DY | DZ, UPPER)
-                arrived(i - 4, DX | DY | DZ, LOWER)
-                pair_message(i - 4, 1, core).start()
-
-            @during(LAST)
-            def _():
-                multiply(i - LAST, 1)
-
-            @pl.when((i >= WINDOW - 1) & (i < n_chunks + WINDOW - 1))
+                    message(s, 8).start()
+
+                pair_message(s, 0, core).start()
+
+            @during(6)
+            def _():
+                arrived(i - 6, DX | DY | DZ, UPPER)
+                arrived(i - 6, DX | DY | DZ, LOWER)
+                pair_message(i - 6, 1, core).start()
+
+            @during(WINDOW - 1)
             def _():
                 drain(i - (WINDOW - 1))
 
             return carry
 
-        lax.fori_loop(0, n_chunks + LAST, step, 0)
-        for c in range(n_chunks + LAST - (WINDOW - 1), n_chunks):
-            drain(c)
+        lax.fori_loop(0, n_parts + LAST, step, 0)
 
 
 def last_kernel(learn_rate, w_up, w_down, g_up, g_down, acc, up_out, down_out, y_ref, result, zeros, sem, zero_sem):
@@ -421,10 +426,10 @@
                 pltpu.VMEM((2, 4, LANES, LANES), BF16),
                 pltpu.VMEM((2, 2, rows, LANES), F32),
                 pltpu.VMEM((2, 2, LANES, rows), F32),
-                pltpu.SemaphoreType.DMA((n_chunks,)),
+                pltpu.SemaphoreType.DMA((2 * n_chunks,)),
                 pltpu.SemaphoreType.DMA((WINDOW, N_SEMS)),
-                pltpu.SemaphoreType.DMA((n_chunks, len(ARRIVALS))),
-                pltpu.SemaphoreType.DMA((n_chunks, 2)),
+                pltpu.SemaphoreType.DMA((2 * n_chunks, len(ARRIVALS))),
+                pltpu.SemaphoreType.DMA((2 * n_chunks, 2)),
                 pltpu.SemaphoreType.DMA((2, 4)),
                 pltpu.SemaphoreType.DMA((2, 4)),
                 pltpu.SemaphoreType.DMA,

time: 200 us -> 200 us (level)
  no operation moved by 1% of the time
where the time goes in v6:
time: 200 us; the launch traced here: 199 us
  Pallas kernels  198 us (99%)
    pallas_call x1, Pallas kernels, local_step(): pl.pallas_call(functools.partial(sync_kernel, n_chunks), out_shape=pltpu....  194 us

profile of v6, /device:TPU:24, one launch (start us, length us, event | category | flops | bytes accessed | tf_op | source)
XLA Modules:
  0.0 199.3 jit_solution(850690384253506230)
XLA Ops:
  1.3 194.3 %shard_map.103.acc = f32[1024,2048]{1,0:T(8,128)S(1)} custom-call(f32[1]{0:T(128)S(6)} %copy.11.learn_rate, f32[1,1,256,2816]{3,2,1,0:T(8,128)} %w_up.3, f32[1,1,2816,256]{3,2,1,0:T(8,128)} %w_down.3, f32[1,1,256,2816]{3,2,1,0:T(8,128)} %g_up.3, f32[1,1,2816,256]{3,2,1,0:T(8,128)} %g_down.3, bf16[1,1,1,2048,2816]{4,3,2,1,0:T(8,128)(2,1)} %old_up.1, ...), custom_call_target="tpu_custom_call" | custom-call | tf_op jit(solution)/shard_map/pallas_call | solution.py:418
  195.6 3.8 %shard_map.104 = (f32[1,1,256,2816]{3,2,1,0:T(8,128)}, f32[1,1,2816,256]{3,2,1,0:T(8,128)}, bf16[1,1,1024,2048]{3,2,1,0:T(8,128)(2,1)}) custom-call(f32[1]{0:T(128)S(6)} %copy.11.learn_rate, f32[1,1,256,2816]{3,2,1,0:T(8,128)} %w_up.3, f32[1,1,2816,256]{3,2,1,0:T(8,128)} %w_down.3, f32[1,1,256,2816]{3,2,1,0:T(8,128)} %g_up.3, f32[1,1,2816,256]{3,2,1,0:T(8,128)} %g_down.3, ...), custom_call_target="tpu_custom_call" | custom-call | tf_op jit(solution)/shard_map/pallas_call | solution.py:443

commit v7 on v6

--- a/solution.py
+++ b/solution.py
@@ -24,8 +24,8 @@
 SENDS = HOP1 + HOP2 + HOP3
 N_SEMS = len(SENDS) + 2
 WINDOW = 10
-PACE = 3
-EARLY = 28
+PACE = 4
+EARLY = 26
 LAST = 9
 VMEM_BYTES = 54 * 2**20
 FINISH = 64
@@ -122,7 +122,7 @@
             def _():
                 pl.semaphore_wait(credit_sem, 1)
 
-            @pl.when((side == 0) & (s >= 1))
+            @pl.when((side == 0) & (s >= 2))
             def _():
                 pl.semaphore_wait(pace_sem, 1)
 
@@ -140,7 +140,7 @@
             def _():
                 delta_copy(s - 1).wait_send()
 
-            @pl.when((side == 1) & (s >= 1))
+            @pl.when((side == 1) & (s >= 1) & (s < n_parts - 1))
             def _():
                 ping(pace_sem, 0, rep)
 

time: 200 us -> 203 us (1.015)
  Pallas kernels: 198 us -> 201 us
    pallas_call x1, Pallas kernels: 194 us -> 198 us  [local_step(): pl.pallas_call(functools.partial(sync_kernel, n_chunks), out_shape=pltpu....]
where the time goes in v7:
time: 203 us
  Pallas kernels  201 us (99%)
    pallas_call x1, Pallas kernels, local_step(): pl.pallas_call(functools.partial(sync_kernel, n_chunks), out_shape=pltpu....  198 us

profile of v7, /device:TPU:24, one launch (start us, length us, event | category | flops | bytes accessed | tf_op | source)
XLA Modules:
  0.0 202.6 jit_solution(15741266931049477987)
XLA Ops:
  1.3 197.5 %shard_map.103.acc = f32[1024,2048]{1,0:T(8,128)S(1)} custom-call(f32[1]{0:T(128)S(6)} %copy.11.learn_rate, f32[1,1,256,2816]{3,2,1,0:T(8,128)} %w_up.3, f32[1,1,2816,256]{3,2,1,0:T(8,128)} %w_down.3, f32[1,1,256,2816]{3,2,1,0:T(8,128)} %g_up.3, f32[1,1,2816,256]{3,2,1,0:T(8,128)} %g_down.3, bf16[1,1,1,2048,2816]{4,3,2,1,0:T(8,128)(2,1)} %old_up.1, ...), custom_call_target="tpu_custom_call" | custom-call | tf_op jit(solution)/shard_map/pallas_call | solution.py:418
  198.8 3.8 %shard_map.104 = (f32[1,1,256,2816]{3,2,1,0:T(8,128)}, f32[1,1,2816,256]{3,2,1,0:T(8,128)}, bf16[1,1,1024,2048]{3,2,1,0:T(8,128)(2,1)}) custom-call(f32[1]{0:T(128)S(6)} %copy.11.learn_rate, f32[1,1,256,2816]{3,2,1,0:T(8,128)} %w_up.3, f32[1,1,2816,256]{3,2,1,0:T(8,128)} %w_down.3, f32[1,1,256,2816]{3,2,1,0:T(8,128)} %g_up.3, f32[1,1,2816,256]{3,2,1,0:T(8,128)} %g_down.3, ...), custom_call_target="tpu_custom_call" | custom-call | tf_op jit(solution)/shard_map/pallas_call | solution.py:443

commit v8 on v5

--- a/solution.py
+++ b/solution.py
@@ -113,9 +113,7 @@
         prompts_in().start()
         ping(barrier, side + 2, rep)
         ping(barrier, 1 - side, rep)
-        for c in (0, 1):
-            prepare(c)
-            fetch(c + 2)
+        prepare(0)
         pl.semaphore_wait(barrier, 2)
 
         def send(c, carry):
@@ -131,11 +129,11 @@
 
             @pl.when(c + 2 < n_chunks)
             def _():
-                prepare(c + 2)
-
-            @pl.when(c + 4 < n_chunks)
-            def _():
-                fetch(c + 4)
+                fetch(c + 2)
+
+            @pl.when(c + 1 < n_chunks)
+            def _():
+                prepare(c + 1)
 
             @pl.when(c >= 1)
             def _():

time: 200 us -> 200 us (level)
  no operation moved by 1% of the time
where the time goes in v8:
time: 200 us
  Pallas kernels  198 us (99%)
    pallas_call x1, Pallas kernels, local_step(): pl.pallas_call(functools.partial(sync_kernel, n_chunks), out_shape=pltpu....  195 us

profile of v8, /device:TPU:24, one launch (start us, length us, event | category | flops | bytes accessed | tf_op | source)
XLA Modules:
  0.0 199.7 jit_solution(11872801804391943308)
XLA Ops:
  1.3 194.6 %shard_map.103.acc = f32[1024,2048]{1,0:T(8,128)S(1)} custom-call(f32[1]{0:T(128)S(6)} %copy.11.learn_rate, f32[1,1,256,2816]{3,2,1,0:T(8,128)} %w_up.3, f32[1,1,2816,256]{3,2,1,0:T(8,128)} %w_down.3, f32[1,1,256,2816]{3,2,1,0:T(8,128)} %g_up.3, f32[1,1,2816,256]{3,2,1,0:T(8,128)} %g_down.3, bf16[1,1,1,2048,2816]{4,3,2,1,0:T(8,128)(2,1)} %old_up.1, ...), custom_call_target="tpu_custom_call" | custom-call | tf_op jit(solution)/shard_map/pallas_call | solution.py:411
  195.9 3.8 %shard_map.104 = (f32[1,1,256,2816]{3,2,1,0:T(8,128)}, f32[1,1,2816,256]{3,2,1,0:T(8,128)}, bf16[1,1,1024,2048]{3,2,1,0:T(8,128)(2,1)}) custom-call(f32[1]{0:T(128)S(6)} %copy.11.learn_rate, f32[1,1,256,2816]{3,2,1,0:T(8,128)} %w_up.3, f32[1,1,2816,256]{3,2,1,0:T(8,128)} %w_down.3, f32[1,1,256,2816]{3,2,1,0:T(8,128)} %g_up.3, f32[1,1,2816,256]{3,2,1,0:T(8,128)} %g_down.3, ...), custom_call_target="tpu_custom_call" | custom-call | tf_op jit(solution)/shard_map/pallas_call | solution.py:436
